TPU v7x, 128 devices: a 2x2x16 block of a 8x8x16 slice. The times are simulated.
128 devices in a mesh: groups: 4 (over x, y), tensor: 32 (over z, core).
Axes of the slice: x: 2, y: 2, z: 16, core: 2. Of those that a mesh axis runs over, the one named last changes fastest.
The devices are a block of a 8x8x16 slice.
Arguments:
- hidden_in: bfloat16 [1024, 8192], P(('groups', 'tensor')), parts along dimension 0, may hold values from -6 to 6
- norm_gain: bfloat16 [8192], replicated, may hold values from 0.25 to 1.75
- w_query: bfloat16 [8192, 64, 128], P(None, 'tensor'), may hold values from -0.0625 to 0.0625
- w_kv: bfloat16 [8192, 8, 2, 128], P('tensor'), may hold values from -0.5 to 0.5
- w_out: bfloat16 [64, 128, 8192], P('tensor'), may hold values from -0.0625 to 0.0625
- prefix_keys: bfloat16 [128, 6, 2048, 128], P(('groups', 'tensor')), parts along dimension 0, may hold values from -1000 to 1000
- prefix_values: bfloat16 [128, 6, 2048, 128], P(('groups', 'tensor')), parts along dimension 0, may hold values from -6 to 6
- suffix_keys: bfloat16 [128, 126, 256, 128], P(('groups', 'tensor')), parts along dimension 0, may hold values from -10 to 10
- suffix_values: bfloat16 [128, 126, 256, 128], P(('groups', 'tensor')), parts along dimension 0, may hold values from -6 to 6
- row_counts: int32 [96], P('groups'), parts along dimension 0, may hold values from 1 to 21, 256 in all
- suffix_lengths: int32 [1024], P('groups'), parts along dimension 0, may hold values from 1 to 256
Outputs:
- layer_out: bfloat16 [1024, 8192], P(('groups', 'tensor')), parts along dimension 0
There are 4 independent parts, one for each index of `groups`. A program takes and returns all parts, laid end to end along the dimension named above; an argument that names none is the same for every part. Nothing has to cross between parts.
Inputs may be any that keep to these rules, and one draw needn't show every extreme that they name: `row_counts`: critique rows are stored prompt by prompt: the rows of prompt p follow those of prompts 0 to p - 1. The counts sum to 256, and some prompt has exactly 21 rows.
All inputs are finite; a program needn't handle non-finite values.
Results may differ from a plain program's by a relative error of at most 0.023.
The roundings to bfloat16 on the way count: a program that leaves them out, or rounds other values in their place, can miss the bound.
Values may be sent and summed in bfloat16 or wider, within the bound.
A program may use at most 128 MiB of HBM per device.

v0:
```python
import math

import jax
import jax.numpy as jnp
from jax import lax
from jax.sharding import Mesh
from jax.sharding import PartitionSpec as P

D = 8192
KVH = 8
HQG = 8
HD = 128
PREFIX = 2048
SMAX = 256
PROM_DEV = 6
PCAP = 21
SLOTS = 126
TENSOR = ("tensor_0", "tensor_1")
GROUPS_TENSOR = ("groups", "tensor_0", "tensor_1")


def sum_in_order(blocks, axes, sequence):
    inside = blocks.shape[1:]
    blocks = blocks.reshape(*(lax.axis_size(a) for a in axes), *inside)
    blocks = jnp.moveaxis(blocks, sequence, range(len(axes))).reshape(-1, *inside)
    for k in sequence:
        blocks = lax.psum_scatter(blocks, axes[k], scatter_dimension=0, tiled=True)
    return blocks[0]


def split_up(value, dim, count):
    before, after = (value.shape[:dim], value.shape[dim + 1 :])
    return jnp.moveaxis(value.reshape(*before, count, -1, *after), dim, 0)


def scatter_axes(value, axes, sequence, dim):
    count = lax.axis_size(axes)
    return sum_in_order(split_up(value, dim, count), axes, sequence)


def rotate(vector, angle):
    half_size = vector.shape[-1] // 2
    front_half = vector[..., :half_size]
    back_half = vector[..., half_size:]
    cosines = jnp.cos(angle)
    sine_terms = jnp.sin(angle)
    return jnp.concatenate(
        [
            front_half * cosines - back_half * sine_terms,
            back_half * cosines + front_half * sine_terms,
        ],
        axis=-1,
    )


def rotation_angles(positions, head_size):
    frequency = 500000.0 ** (-(2.0 * jnp.arange(head_size // 2, dtype=jnp.float32)) / head_size)
    return positions.astype(jnp.float32)[:, None] * frequency[None, :]


def attend_prompt(inputs):
    query_block, key_new, value_new, past_keys, past_values, tail_keys, tail_values, lengths = (
        inputs
    )
    slot_count, head_count, head_size = query_block.shape
    scaling = 1.0 / math.sqrt(head_size)
    flattened = query_block.reshape(slot_count * head_count, head_size)
    prefix_scores = jnp.einsum(
        "qd,td->qt", flattened, past_keys, preferred_element_type=jnp.float32
    )
    prefix_scores = prefix_scores.reshape(slot_count, head_count, past_keys.shape[0]) * scaling
    suffix_scores = (
        jnp.einsum("rjd,rtd->rjt", query_block, tail_keys, preferred_element_type=jnp.float32)
        * scaling
    )
    visible = jnp.arange(tail_keys.shape[1])[None, :] < lengths[:, None]
    suffix_scores = jnp.where(visible[:, None, :], suffix_scores, -jnp.inf)
    self_score = (
        jnp.einsum("rjd,rd->rj", query_block, key_new, preferred_element_type=jnp.float32) * scaling
    )
    highest = jnp.maximum(
        jnp.max(prefix_scores, axis=2), jnp.maximum(jnp.max(suffix_scores, axis=2), self_score)
    )
    prefix_exp = jnp.exp(prefix_scores - highest[..., None])
    suffix_exp = jnp.exp(suffix_scores - highest[..., None])
    self_exp = jnp.exp(self_score - highest)
    totals = jnp.sum(prefix_exp, axis=2) + jnp.sum(suffix_exp, axis=2) + self_exp
    prefix_weights = (prefix_exp / totals[..., None]).astype(jnp.bfloat16)
    suffix_weights = (suffix_exp / totals[..., None]).astype(jnp.bfloat16)
    self_weight = (self_exp / totals).astype(jnp.bfloat16)
    combined = jnp.dot(
        prefix_weights.reshape(slot_count * head_count, -1),
        past_values,
        preferred_element_type=jnp.float32,
    )
    combined = combined.reshape(slot_count, head_count, head_size)
    combined = combined + jnp.einsum(
        "rjt,rtd->rjd", suffix_weights, tail_values, preferred_element_type=jnp.float32
    )
    combined = (
        combined
        + self_weight.astype(jnp.float32)[..., None] * value_new.astype(jnp.float32)[:, None, :]
    )
    return combined.astype(jnp.bfloat16)


def local(
    hidden_in,
    norm_gain,
    w_query,
    w_kv,
    w_out,
    prefix_keys,
    prefix_values,
    suffix_keys,
    suffix_values,
    row_counts,
    suffix_lengths,
):
    devices = lax.axis_size(TENSOR)
    my_index = lax.axis_index(TENSOR)
    my_group = my_index // KVH
    my_head = my_index % KVH
    head_share = w_query.shape[1]
    holders = HQG // head_share
    slab = w_kv.shape[0]
    rows_all = suffix_lengths.shape[0]
    groups = devices // KVH
    prompts = row_counts.shape[0]
    widened = hidden_in.astype(jnp.float32)
    inverse_norm = lax.rsqrt(jnp.mean(widened * widened, axis=1, keepdims=True) + 1e-05)
    normed = (widened * inverse_norm * norm_gain.astype(jnp.float32)[None, :]).astype(jnp.bfloat16)
    query_cols = w_query.reshape(D, head_share * HD)
    kv_rows = w_kv.reshape(slab, KVH * 2 * HD)
    rows_piece = lax.all_gather(normed, TENSOR, axis=0, tiled=True)
    own_heads = jnp.dot(rows_piece, query_cols, preferred_element_type=jnp.float32)
    features = lax.dynamic_slice_in_dim(rows_piece, my_index * slab, slab, 1)
    partial_kv = jnp.dot(features, kv_rows, preferred_element_type=jnp.float32)
    projected = jnp.concatenate([own_heads, partial_kv], axis=1)
    my_queries = (
        projected[:, : head_share * HD].astype(jnp.bfloat16).reshape(rows_all, head_share, HD)
    )
    kv_partial = projected[:, head_share * HD :]
    row_ends = jnp.cumsum(row_counts)
    row_starts = row_ends - row_counts
    slot_rows = jnp.minimum(
        row_starts[:, None] + jnp.arange(PCAP, dtype=jnp.int32)[None, :], rows_all - 1
    )
    slot_flat = slot_rows.reshape(prompts * PCAP)
    own_rows = lax.dynamic_slice_in_dim(slot_rows, my_group * PROM_DEV, PROM_DEV, 0).reshape(SLOTS)
    kv_slots = kv_partial[slot_flat].reshape(groups, SLOTS, KVH, 2 * HD).transpose(0, 2, 1, 3)
    kv_slots = kv_slots.reshape(devices, SLOTS, 2 * HD)
    kv_mine = scatter_axes(kv_slots, TENSOR, (1, 0), 0)
    kv_mine = kv_mine.astype(jnp.bfloat16).reshape(SLOTS, 2, HD)
    complete = lax.all_gather(my_queries, TENSOR, axis=1, tiled=True)
    gathered = lax.dynamic_slice_in_dim(complete[own_rows], my_head * HQG, HQG, 1)
    lengths = suffix_lengths[own_rows]
    rotation = rotation_angles(PREFIX + lengths, HD)
    queries = rotate(gathered.astype(jnp.float32), rotation[:, None, :]).astype(jnp.bfloat16)
    key_new = rotate(kv_mine[:, 0].astype(jnp.float32), rotation).astype(jnp.bfloat16)
    value_new = kv_mine[:, 1]
    blocks = (
        queries.reshape(PROM_DEV, PCAP, HQG, HD),
        key_new.reshape(PROM_DEV, PCAP, HD),
        value_new.reshape(PROM_DEV, PCAP, HD),
        prefix_keys[0],
        prefix_values[0],
        suffix_keys[0].reshape(PROM_DEV, PCAP, SMAX, HD),
        suffix_values[0].reshape(PROM_DEV, PCAP, SMAX, HD),
        lengths.reshape(PROM_DEV, PCAP),
    )
    attended = lax.map(attend_prompt, blocks).reshape(SLOTS, HQG, HD)
    wanted_head = my_index // holders
    head_offset = my_index % holders * head_share
    everything = lax.all_gather(attended[None], TENSOR, axis=0, tiled=True)
    picked = everything.reshape(groups, KVH, SLOTS, HQG, HD)
    picked = lax.dynamic_index_in_dim(picked, wanted_head, 1, keepdims=False)
    slot_table = lax.dynamic_slice_in_dim(picked, head_offset, head_share, 2)
    slot_table = slot_table.reshape(prompts * PCAP, head_share * HD)
    row_index = jnp.arange(rows_all, dtype=jnp.int32)
    prompt_of = jnp.sum((row_index[:, None] >= row_ends[None, :]).astype(jnp.int32), axis=1)
    row_slot = prompt_of * PCAP + (row_index - row_starts[prompt_of])
    row_outputs = slot_table[row_slot]
    out_weight = w_out.reshape(head_share * HD, D)
    summed = scatter_axes(
        jnp.dot(row_outputs, out_weight, preferred_element_type=jnp.float32).astype(jnp.bfloat16),
        TENSOR,
        (1, 0),
        0,
    ).astype(jnp.float32)
    return (widened + summed).astype(jnp.bfloat16)


def solution(mesh):
    split = Mesh(
        mesh.devices.reshape(mesh.shape["groups"], 16, 2), ("groups", "tensor_0", "tensor_1")
    )
    return jax.shard_map(
        local,
        mesh=split,
        in_specs=(
            P(GROUPS_TENSOR, None),
            P(),
            P(None, TENSOR, None),
            P(TENSOR, None, None, None),
            P(TENSOR, None, None),
            P(GROUPS_TENSOR, None, None, None),
            P(GROUPS_TENSOR, None, None, None),
            P(GROUPS_TENSOR, None, None, None),
            P(GROUPS_TENSOR, None, None, None),
            P("groups"),
            P("groups"),
        ),
        out_specs=P(GROUPS_TENSOR, None),
        check_vma=False,
    )
```

profile of v0, /device:TPU:86, one launch (start us, length us, event | category | flops | bytes accessed | tf_op | source)
XLA Modules:
  0.0 481.5 jit_solution(605796550187949551)
XLA Ops:
  8.4 1.7 fusion.59
  10.2 76.1 %all-gather.4.cloned.1.call-done = bf16[256,8192]{1,0:T(8,128)(2,1)} async-done(((bf16[8,8192]{1,0:T(8,128)(2,1)}), bf16[256,8192]{1,0:T(8,128)(2,1)}) %all-gather.4.cloned.1.call-update) | async-done | bytes 4194320 | tf_op jit(solution)/shard_map/all_gather | solution.py:135
  86.2 5.3 %fusion.54 = bf16[256,256]{0,1:T(8,128)(2,1)S(1)} fusion(bf16[256,8192]{1,0:T(8,128)(2,1)} %all-gather.4.cloned.1.call-done, bf16[1024,8,2,128]{3,2,1,0:T(2,128)(2,1)} %bitcast.199), kind=kOutput, calls=%fused_computation.59 | convolution fusion | flops 1073807360 | bytes 8519680 | tf_op jit(solution)/shard_map/dot_general | solution.py:136
  93.7 1.3 fusion.61
  95.1 3.6 gather_fusion.2
  98.7 4.1 copy.69
  102.8 1.3 copy.57
  104.1 4.3 copy.58
  108.9 1.3 gather_fusion.1
  110.9 48.5 %all-gather.6.cloned.1.call-done = bf16[256,64,128]{2,0,1:T(8,128)(2,1)} async-done(((bf16[256,2,128]{2,0,1:T(8,128)(2,1)}), bf16[256,64,128]{2,0,1:T(8,128)(2,1)}) %all-gather.6.cloned.1.call-update) | async-done | bytes 4194320 | tf_op jit(solution)/shard_map/all_gather | solution.py:155
  159.4 6.9 %copy.54 = bf16[256,64,128]{2,1,0:T(8,128)(2,1)} copy(bf16[256,64,128]{2,0,1:T(8,128)(2,1)} %all-gather.6.cloned.1.call-done) | data formatting | bytes 8388608 | tf_op jit(solution)/shard_map/all_gather | solution.py:155
  166.3 3.1 gather_fusion
  169.5 9.4 %reduce-scatter.5.cloned.1.call-done = f32[16,1,126,256]{3,0,2,1:T(8,128)} async-done(((f32[32,1,126,256]{3,0,2,1:T(8,128)}), f32[16,1,126,256]{3,0,2,1:T(8,128)}) %reduce-scatter.5.cloned.1.call-update) | async-done | bytes 2064400 | tf_op jit(solution)/shard_map/reduce_scatter | solution.py:27
  178.9 76.8 %all-reduce.2 = bf16[16,1,126,256]{3,0,2,1:T(8,128)(2,1)S(1)} all-reduce(f32[16,1,126,256]{3,0,2,1:T(8,128)} %reduce-scatter.5.cloned.1.call-done), channel_id=3, replica_groups=mesh['groups'=4,'tensor_0'=16,'tensor_1'=2] {'tensor_0'}, use_global_device_ids=true, to_apply=%region_3.4.clone | all-reduce | flops 516096 | bytes 3096576
  258.0 44.4 %while.10 = (s32[]{:T(128)}, bf16[6,21,8,128]{3,2,1,0:T(8,128)(2,1)S(1)}, bf16[6,21,8,128]{3,2,1,0:T(8,128)(2,1)S(1)}, bf16[6,2048,128]{2,1,0:T(8,128)(2,1)}, s3...) while((s32[]{:T(128)}, ...), condition=%wide.region_9.10_spmd, body=%wide.region_4.9_spmd.sunk | while | flops 201071472 | bytes 8900441 | solution.py:172
  258.1 1.9 fusion.94
  260.2 1.5 fusion.92
  262.2 1.4 fusion.99
  263.7 1.7 fusion.100
  265.5 1.9 fusion.94
  267.6 1.5 fusion.92
  269.6 1.4 fusion.99
  271.1 1.7 fusion.100
  272.9 1.9 fusion.94
  275.0 1.5 fusion.92
  277.0 1.4 fusion.99
  278.5 1.7 fusion.100
  280.3 1.9 fusion.94
  282.4 1.5 fusion.92
  284.4 1.4 fusion.99
  285.9 1.7 fusion.100
  287.7 1.9 fusion.94
  289.8 1.5 fusion.92
  291.8 1.4 fusion.99
  293.3 1.7 fusion.100
  295.1 1.9 fusion.94
  297.2 1.5 fusion.92
  299.2 1.4 fusion.99
  300.7 1.7 fusion.100
  304.8 4.5 compare_select_fusion.3
  309.3 10.5 %select_select_fusion = s32[256]{0:T(256)S(1)} fusion(pred[256]{0:T(512)(128)(4,1)S(1)} %get-tuple-element.84, pred[256]{0:T(512)(128)(4,1)S(1)} %get-tuple-element.83, pred[256]{0:T(512)(128)(4,1)S(1)} %get-tuple-element.82, pred[256]{0:T(512)(128)(4,1)S(1)} %get-tuple-element.81, pred[256]{0:T(512)(128)(4,1)S(1)} %get-tuple-element.80, ...), kind=kLoop, calls=%fused_computation.115 | loop fusion | flops 4352 | bytes 6468 | tf_op jit(solution)/shard_map/gather | solution.py:182
  319.9 54.5 %all-gather.8.cloned.1.call-done = bf16[32,126,8,128]{3,2,1,0:T(8,128)(2,1)} async-done(((bf16[1,126,8,128]{3,2,1,0:T(8,128)(2,1)}), bf16[32,126,8,128]{3,2,1,0:T(8,128)(2,1)}) %all-gather.8.cloned.1.call-update) | async-done | bytes 8257552 | tf_op jit(solution)/shard_map/all_gather | solution.py:175
  374.4 1.5 constant_dynamic-slice_fusion.1
  377.1 3.4 convolution_convert_fusion
  380.6 2.2 copy.63
  382.9 16.6 %reduce-scatter.7.cloned.1.call-done = bf16[16,8,8192]{2,1,0:T(8,128)(2,1)} async-done(((bf16[32,8,8192]{2,1,0:T(8,128)(2,1)}), bf16[16,8,8192]{2,1,0:T(8,128)(2,1)}) %reduce-scatter.7.cloned.1.call-update) | async-done | bytes 2097168 | tf_op jit(solution)/shard_map/reduce_scatter | solution.py:27
  399.6 73.4 %reduce-scatter.9.cloned.1.call-done = bf16[1,8,8192]{2,1,0:T(8,128)(2,1)} async-done(((bf16[16,8,8192]{2,1,0:T(8,128)(2,1)}), bf16[1,8,8192]{2,1,0:T(8,128)(2,1)}) %reduce-scatter.9.cloned.1.call-update) | async-done | bytes 131088 | tf_op jit(solution)/shard_map/reduce_scatter | solution.py:27
  473.0 1.6 fusion.60
  (126 shorter events, 16.2 us)
Async XLA Ops:
  6.5 102.3 %copy-start = (s32[256]{0:T(256)S(1)}, s32[256]{0:T(256)}, u32[]{:S(2)}) copy-start(s32[256]{0:T(256)} %param.23) | copy-start | bytes 3076
  6.6 79.7 %all-gather.4.cloned.1.call-start = ((), (), s32[]{:S(2)}) async-start(), calls=%async_computation.3 | async-start | bytes 4325376 | tf_op jit(solution)/shard_map/all_gather | solution.py:135
  10.1 149.3 %all-gather.6.cloned.1.call-start = ((), (), s32[]{:S(2)}) async-start(), calls=%async_computation.4 | async-start | bytes 4325376 | tf_op jit(solution)/shard_map/all_gather | solution.py:155
  86.2 6.2 %copy-start.5 = (s32[24]{0:T(128)S(1)}, s32[24]{0:T(128)}, u32[]{:S(2)}) copy-start(s32[24]{0:T(128)} %param.22) | copy-start | bytes 292
  86.2 6.5 %copy-start.3 = (bf16[256,8,2,128]{3,2,1,0:T(2,128)(2,1)S(1)}, bf16[256,8,2,128]{3,2,1,0:T(2,128)(2,1)}, u32[]{:S(2)}) copy-start(bf16[256,8,2,128]{3,2,1,0:T(2,128)(2,1)} %param.16) | copy-start | bytes 3145732
  92.3 86.5 %reduce-scatter.5.cloned.1.call-start = ((), (), s32[]{:S(2)}) async-start(), calls=%async_computation.5 | async-start | bytes 6193152 | tf_op jit(solution)/shard_map/reduce_scatter | solution.py:27
  108.4 1.8 copy-start.6
  108.5 266.0 %all-gather.8.cloned.1.call-start = ((), (), s32[]{:S(2)}) async-start(), calls=%async_computation.6 | async-start | bytes 8515584 | tf_op jit(solution)/shard_map/all_gather | solution.py:175
  302.4 0.8 copy-start.4
  303.2 96.3 %reduce-scatter.7.cloned.1.call-start = ((), (), s32[]{:S(2)}) async-start(), calls=%async_computation.7 | async-start | bytes 6291456 | tf_op jit(solution)/shard_map/reduce_scatter | solution.py:27
  380.6 94.1 %copy-start.1 = (s32[256]{0:T(256)S(1)}, s32[256]{0:T(256)}, u32[]{:S(2)}) copy-start(s32[256]{0:T(256)} %param.23) | copy-start | bytes 3076
  382.8 90.2 %copy-start.2 = (bf16[8,8192]{1,0:T(8,128)(2,1)S(1)}, bf16[8,8192]{1,0:T(8,128)(2,1)}, u32[]{:S(2)}) copy-start(bf16[8,8192]{1,0:T(8,128)(2,1)} %param.13) | copy-start | bytes 393220
  382.9 90.2 %reduce-scatter.9.cloned.1.call-start = ((), (), s32[]{:S(2)}) async-start(), calls=%async_computation.8 | async-start | bytes 2228224 | tf_op jit(solution)/shard_map/reduce_scatter | solution.py:27
Sparse Core Ops, SparseCore 0:
  10.2 75.9 all-gather.3
  92.5 66.9 all-gather.5
  161.9 16.9 reduce-scatter.4
  303.3 71.0 all-gather.7
  383.0 16.5 reduce-scatter.6
  401.8 71.1 reduce-scatter.8
where the time goes:
time: 484 us; the launch traced here: 481 us
  waiting for transfers between devices  279 us (58%)
  blocking collectives  76.8 us (16%)
  matrix products  50.3 us (10%)
  local copies, waits for them, and re-layouts  35.8 us (7%)
  other arithmetic  25.1 us (5%)
  between operations  13.9 us (3%)
    reduce_scatter x3, waiting for transfers between devices, sum_in_order(): blocks = lax.psum_scatter(blocks, axes[k], scatter_dimension=0, tiled=True)  99.4 us
    unnamed x1, blocking collectives  76.8 us
    all_gather x1, waiting for transfers between devices, local(): rows_piece = lax.all_gather(normed, TENSOR, axis=0, tiled=True)  76.1 us
    all_gather x1, waiting for transfers between devices, local(): everything = lax.all_gather(attended[None], TENSOR, axis=0, tiled=True)  54.5 us
    all_gather x1, waiting for transfers between devices, local(): complete = lax.all_gather(my_queries, TENSOR, axis=1, tiled=True)  48.5 us
    gather x3, other arithmetic, local(): row_slot = prompt_of * PCAP + (row_index - row_starts[prompt_of])  15.1 us
    dot_general x6, matrix products, attend_prompt(): jnp.einsum('rjd,rtd->rjt', query_block, tail_keys, preferred_element_type...  11.3 us
    dot_general x6, matrix products, attend_prompt(): jnp.einsum('rjt,rtd->rjd', suffix_weights, tail_values, preferred_element...  10.3 us
  transfers between devices with their start and end apart: 6, of which 6 were waited for; matrix products, arithmetic and copies ran while one was open for 9% of the time, Pallas kernels for 0%

commit v1 on v0

v1 whole, which is shorter than its diff:
```python
import functools
import math

import jax
import jax.numpy as jnp
from jax import lax
from jax.experimental import pallas as pl
from jax.experimental.pallas import tpu as pltpu
from jax.sharding import Mesh
from jax.sharding import PartitionSpec as P

HD = 128
PREFIX = 2048
PCAP = 21
PAD = 128
TENSOR = ("tensor_0", "tensor_1")
GROUPS_TENSOR = ("groups", "tensor_0", "tensor_1")
MESH = pl.DeviceIdType.MESH
KVT = jnp.float32
XCH = 4
RCH = 8
F32 = jnp.float32
BF16 = jnp.bfloat16


def at(z, c):
    return {"tensor_0": z, "tensor_1": c}


def remote(src, dst, send, recv, z, c):
    return pltpu.make_async_remote_copy(
        src_ref=src, dst_ref=dst, send_sem=send, recv_sem=recv, device_id=at(z, c), device_id_type=MESH
    )


def project_kernel(
    chips, hidden, gain, wq_hbm, wkv_hbm, cosf, sinf, slots, q_out, kv_out,
    x, wq, wkv, kvs, kvr, qs, kvh, kvl,
    wq_sem, wkv_sem, wkvs_sem, wkvr_sem, xs, xr, ps, pr, ks, kr, qss, qrs, qls, as_, ar, al,
):
    z = lax.axis_index("tensor_0")
    c = lax.axis_index("tensor_1")
    devices = 2 * chips
    half = chips // 2
    me = 2 * z + c
    right = lax.rem(z + 1, chips)
    left = lax.rem(z + chips - 1, chips)
    slab = wkv_hbm.shape[0]
    width = x.shape[2] // XCH
    barrier = pltpu.get_barrier_semaphore()

    def greet(n, carry):
        @pl.when(n != me)
        def _():
            pl.semaphore_signal(barrier, inc=1, device_id=at(n // 2, lax.rem(n, 2)), device_id_type=MESH)

        return carry

    lax.fori_loop(0, devices, greet, 0)
    load_wq = pltpu.make_async_copy(wq_hbm, wq, wq_sem)
    load_wq.start()
    own_rows = pl.ds(pl.multiple_of(c * slab, slab), slab)
    load_wkv = pltpu.make_async_copy(wkv_hbm, wkv.at[own_rows, :], wkv_sem)
    load_wkv.start()

    wide = hidden[...].astype(F32)
    inverse = lax.rsqrt(jnp.mean(wide * wide, axis=1, keepdims=True) + 1e-05)
    x[me] = (wide * inverse * gain[...].astype(F32)).astype(BF16)
    kvs[1, 0] = jnp.zeros(kvs.shape[2:], kvs.dtype)

    pl.semaphore_wait(barrier, devices - 1)

    send_wkv = remote(wkv_hbm, wkv.at[own_rows, :], wkvs_sem, wkvr_sem, z, 1 - c)
    send_wkv.start()

    def row_copy(way, step, j, shard):
        piece = x.at[shard, :, pl.ds(j * width, width)]
        return remote(piece, piece, xs.at[way, step, j], xr.at[way, step, j], right if way == 0 else left, c)

    def part_copy(way, step, shard):
        return remote(x.at[shard], x.at[shard], ps.at[way, step], pr.at[way, step], z, 1 - c)

    def kv_copy(way, step):
        return remote(kvs.at[way, step], kvr.at[way, step], ks.at[way, step], kr.at[way, step], right if way == 0 else left, c)

    for j in range(XCH):
        row_copy(0, 0, j, me).start()
        row_copy(1, 0, j, me).start()
    part_copy(0, 0, me).start()
    kv_copy(1, 0).start()
    feats = pl.ds(pl.multiple_of(z * 2 * slab, 2 * slab), 2 * slab)

    load_wkv.wait()
    send_wkv.wait()
    own = jnp.dot(x[me, :, feats], wkv[...], preferred_element_type=F32)
    kvs[0, 0] = own.astype(kvs.dtype)
    kv_copy(0, 0).start()

    def hop(s, carry):
        cw = 2 * lax.rem(z - s + chips, chips) + c
        ccw = 2 * lax.rem(z + s, chips) + c
        for j in range(XCH):
            row_copy(0, s - 1, j, cw).wait_recv()
            row_copy(0, s, j, cw).start()
            row_copy(1, s - 1, j, ccw).wait_recv()

            @pl.when(s < half - 1)
            def _():
                row_copy(1, s, j, ccw).start()

        part_copy(0, s, cw).start()
        part_copy(1, s, ccw).start()
        both = jnp.concatenate([x[cw, :, feats].astype(F32), x[ccw, :, feats].astype(F32)], axis=0).astype(BF16)
        part = jnp.dot(both, wkv[...], preferred_element_type=F32)
        kv_copy(0, s - 1).wait_recv()
        kvs[0, s] = (part[:8] + kvr[0, s - 1].astype(F32)).astype(kvs.dtype)
        kv_copy(0, s).start()
        kv_copy(1, s - 1).wait_recv()
        kvs[1, s] = (part[8:] + kvr[1, s - 1].astype(F32)).astype(kvs.dtype)
        kv_copy(1, s).start()
        return carry

    lax.fori_loop(1, half, hop, 0)
    far = 2 * lax.rem(z + half, chips) + c
    for j in range(XCH):
        row_copy(0, half - 1, j, far).wait_recv()
    part_copy(0, half, far).start()
    own = jnp.dot(x[far, :, feats], wkv[...], preferred_element_type=F32)
    kv_copy(0, half - 1).wait_recv()
    kv_copy(1, half - 1).wait_recv()
    kv_raw = (own + kvr[0, half - 1].astype(F32) + kvr[1, half - 1].astype(F32)).astype(BF16).astype(F32)
    far_rows = pl.ds(pl.multiple_of(far * 8, 8), 8)
    cos8 = cosf[far_rows, :]
    sin8 = sinf[far_rows, :]
    heads = kvh.shape[0]
    for h in range(heads):
        key = kv_raw[:, h * 2 * HD : h * 2 * HD + HD]
        value = kv_raw[:, h * 2 * HD + HD : (h + 1) * 2 * HD]
        kvh[h, :, :HD] = (key * cos8 + pltpu.roll(key, HD // 2, 1) * sin8).astype(BF16)
        kvh[h, :, HD:] = value.astype(BF16)

    def kv_send(n):
        return remote(kvh.at[lax.rem(n, heads)], kvl.at[far], as_.at[n], ar.at[far], n // 2, lax.rem(n, 2))

    kv_self = pltpu.make_async_copy(kvh.at[lax.rem(me, heads)], kvl.at[far], al)

    def kv_out_loop(n, carry):
        @pl.when(n != me)
        def _():
            kv_send(n).start()

        return carry

    lax.fori_loop(0, devices, kv_out_loop, 0)
    kv_self.start()

    part_copy(0, 0, 2 * z + 1 - c).wait_recv()

    def part_wait(s, carry):
        part_copy(0, s, me).wait_recv()
        part_copy(1, s, me).wait_recv()
        return carry

    lax.fori_loop(1, half, part_wait, 0)
    part_copy(0, half, me).wait_recv()
    load_wq.wait()
    depth = 1024
    rows = devices * 8

    def q_step(k, acc):
        piece = pl.ds(pl.multiple_of(k * depth, depth), depth)
        xk = x[:, :, piece].astype(F32).reshape(rows, depth).astype(BF16)
        return acc + jnp.dot(xk, wq[piece, :], preferred_element_type=F32)

    acc = lax.fori_loop(0, x.shape[2] // depth, q_step, jnp.zeros((rows, 2 * HD), F32))
    q_raw = acc.astype(BF16).astype(F32)
    roped = []
    for j in range(2):
        v = q_raw[:, j * HD : (j + 1) * HD]
        roped.append((v * cosf[...] + pltpu.roll(v, HD // 2, 1) * sinf[...]).astype(BF16))
    roped = jnp.concatenate(roped, axis=1)
    groups = qs.shape[0]
    hit = lax.broadcasted_iota(jnp.int32, (groups * PAD, rows), 1) == slots[...]
    pick = jnp.where(hit, 1.0, 0.0).astype(BF16)
    picked = jnp.dot(pick, roped, preferred_element_type=F32).astype(BF16)
    block = 2 * lax.rem(z, 2) + c
    my_head = lax.rem(me, heads)

    def q_send(g):
        owner = heads * g + z // 2
        return remote(qs.at[g], q_out.at[block], qss.at[g], qrs.at[block], owner // 2, lax.rem(owner, 2))

    def q_local(g):
        return pltpu.make_async_copy(qs.at[g], q_out.at[block], qls)

    for g in range(groups):
        qs[g] = picked[g * PAD : (g + 1) * PAD]
        owner = heads * g + z // 2

        @pl.when(owner != me)
        def _():
            q_send(g).start()

        @pl.when(owner == me)
        def _():
            q_local(g).start()

    def kv_in_loop(n, carry):
        @pl.when(n != far)
        def _():
            remote(kvh.at[0], kvl.at[n], as_.at[0], ar.at[n], z, 1 - c).wait_recv()

        return carry

    lax.fori_loop(0, devices, kv_in_loop, 0)
    kv_self.wait()
    mine = slots[pl.ds(pl.multiple_of(z // (heads // 2) * PAD, PAD), PAD), :]
    hit = lax.broadcasted_iota(jnp.int32, (PAD, rows), 1) == mine
    pick = jnp.where(hit, 1.0, 0.0).astype(BF16)
    table = kvl[...].astype(F32).reshape(rows, 2 * HD).astype(BF16)
    kv_out[...] = jnp.dot(pick, table, preferred_element_type=F32).astype(BF16)

    for b in range(groups):
        source = groups * my_head + b

        @pl.when(source != me)
        def _():
            remote(qs.at[0], q_out.at[b], qss.at[0], qrs.at[b], z, 1 - c).wait_recv()

    for g in range(groups):
        owner = heads * g + z // 2

        @pl.when(owner == me)
        def _():
            q_local(g).wait()

        @pl.when(owner != me)
        def _():
            q_send(g).wait_send()

    for j in range(XCH):
        row_copy(0, 0, j, me).wait_send()
        row_copy(1, 0, j, me).wait_send()
    part_copy(0, 0, me).wait_send()
    kv_copy(0, 0).wait_send()
    kv_copy(1, 0).wait_send()

    def drain(s, carry):
        for j in range(XCH):
            row_copy(0, s, j, me).wait_send()

            @pl.when(s < half - 1)
            def _():
                row_copy(1, s, j, me).wait_send()

        part_copy(0, s, me).wait_send()
        part_copy(1, s, me).wait_send()
        kv_copy(0, s).wait_send()
        kv_copy(1, s).wait_send()
        return carry

    lax.fori_loop(1, half, drain, 0)
    part_copy(0, half, me).wait_send()

    def kv_drain(n, carry):
        @pl.when(n != me)
        def _():
            kv_send(n).wait_send()

        return carry

    lax.fori_loop(0, devices, kv_drain, 0)


def attend_kernel(lens, q, kv, pk, pv, sk, sv, out, qf, kf, vf, ss, pvacc, att):
    i = pl.program_id(0)
    scaling = 1.0 / math.sqrt(HD)
    per = qf.shape[0] // PAD
    rows = PCAP * per

    @pl.when(i == 0)
    def _():
        key = kv[:, :HD].astype(F32)
        value = kv[:, HD:].astype(F32)
        for j in range(per):
            qf[pl.ds(j, PAD, stride=per), :] = q[j // 2, :, (j % 2) * HD : (j % 2 + 1) * HD].astype(F32)
            kf[pl.ds(j, PAD, stride=per), :] = key
            vf[pl.ds(j, PAD, stride=per), :] = value
        att[...] = jnp.zeros_like(att)

    mine = pl.ds(pl.multiple_of(i * rows, 8), rows)
    qi = qf[mine, :]
    qb = qi.astype(BF16)
    contract = (((1,), (1,)), ((), ()))
    ps = lax.dot_general(qb, pk[0], contract, preferred_element_type=F32) * scaling
    for r in range(PCAP):
        q8 = qf[pl.ds(pl.multiple_of(i * rows + r * per, 8), per), :].astype(BF16)
        s8 = lax.dot_general(q8, sk[r], contract, preferred_element_type=F32) * scaling
        seen = lax.broadcasted_iota(jnp.int32, s8.shape, 1) < lens[i * PCAP + r]
        ss[r * per : (r + 1) * per, :] = jnp.where(seen, s8, -jnp.inf)
    self_score = jnp.sum(qi * kf[mine, :], axis=1, keepdims=True) * scaling
    sfx = ss[...]
    top = jnp.maximum(jnp.max(ps, axis=1, keepdims=True), jnp.maximum(jnp.max(sfx, axis=1, keepdims=True), self_score))
    pe = jnp.exp(ps - top)
    se = jnp.exp(sfx - top)
    own = jnp.exp(self_score - top)
    total = jnp.sum(pe, axis=1, keepdims=True) + jnp.sum(se, axis=1, keepdims=True) + own
    acc = jnp.dot(pe.astype(BF16), pv[0], preferred_element_type=F32)
    ss[...] = se
    for r in range(PCAP):
        w8 = ss[r * per : (r + 1) * per, :].astype(BF16)
        pvacc[r * per : (r + 1) * per, :] = jnp.dot(w8, sv[r], preferred_element_type=F32)
    acc = acc + pvacc[...] + own * vf[mine, :]
    att[mine, :] = acc / total

    @pl.when(i == pl.num_programs(0) - 1)
    def _():
        for j in range(per):
            out[j // 2, :, (j % 2) * HD : (j % 2 + 1) * HD] = att[pl.ds(j, PAD, stride=per), :].astype(BF16)


def output_kernel(
    chips, hidden, att, wo_hbm, slots, out,
    a, w2, x2, p, rs, rr,
    wo_sem, wos, wor, ass, ars, als, xss, xrs, ss, sr,
):
    z = lax.axis_index("tensor_0")
    c = lax.axis_index("tensor_1")
    devices = 2 * chips
    half = chips // 2
    me = 2 * z + c
    right = lax.rem(z + 1, chips)
    left = lax.rem(z + chips - 1, chips)
    blocks = att.shape[0]
    heads = devices // blocks
    groups = blocks
    my_group = me // heads
    my_head = lax.rem(me, heads)
    width = hidden.shape[1] // RCH
    rows = devices * 8
    barrier = pltpu.get_barrier_semaphore()

    def greet(n):
        pl.semaphore_signal(barrier, inc=1, device_id=at(n // 2, lax.rem(n, 2)), device_id_type=MESH)

    greet(2 * right + c)
    greet(2 * left + c)
    greet(2 * z + 1 - c)
    for g in range(groups):
        source = heads * g + me // blocks

        @pl.when(source != me)
        def _():
            greet(source)

    load = pltpu.make_async_copy(wo_hbm, w2.at[c], wo_sem)
    load.start()
    kept = jnp.where(me // blocks == my_head, 1, 0)
    pl.semaphore_wait(barrier, 3 + blocks - kept)

    def a_send(b):
        dest = blocks * my_head + b
        return remote(att.at[b], a.at[my_group], ass.at[b], ars.at[my_group], dest // 2, lax.rem(dest, 2))

    def a_local(b):
        return pltpu.make_async_copy(att.at[b], a.at[my_group], als)

    for b in range(blocks):
        dest = blocks * my_head + b

        @pl.when(dest != me)
        def _():
            a_send(b).start()

        @pl.when(dest == me)
        def _():
            a_local(b).start()

    send_w = remote(wo_hbm, w2.at[c], wos, wor, z, 1 - c)
    send_w.start()

    for g in range(groups):
        source = heads * g + me // blocks

        @pl.when(source != me)
        def _():
            remote(att.at[0], a.at[g], ass.at[0], ars.at[g], z, 1 - c).wait_recv()

    for b in range(blocks):
        dest = blocks * my_head + b

        @pl.when(dest == me)
        def _():
            a_local(b).wait()

        @pl.when(dest != me)
        def _():
            a_send(b).wait_send()

    order = lax.broadcasted_iota(jnp.int32, (rows, groups * PAD), 0)
    wanted = (lax.rem(order, rows // 2) // 8 * 2 + order // (rows // 2)) * 8 + lax.rem(order, 8)
    pick = jnp.where(wanted == slots[...], 1.0, 0.0).astype(BF16)
    table = a[...].reshape(groups * PAD, 2 * HD)
    picked = jnp.dot(pick, table, preferred_element_type=F32).astype(BF16)
    x2[0, 0] = picked[: rows // 2]
    x2[0, 1] = picked[rows // 2 :]
    swap = remote(x2.at[0, 1 - c], x2.at[1, 0], xss, xrs, z, 1 - c)
    swap.start()
    load.wait()
    send_w.wait()
    swap.wait()

    def ring(way, step, j):
        return remote(rs.at[way, step, j], rr.at[way, step, j], ss.at[way, step, j], sr.at[way, step, j], right if way == 0 else left, c)

    def block_of(chip, cols):
        return p[pl.ds(pl.multiple_of(chip * 8, 8), 8), cols]

    far = lax.rem(z + half, chips)
    far_left = lax.rem(z + half + 1, chips)
    for j in range(RCH):
        cols = pl.ds(j * width, width)
        first = jnp.dot(x2[0, c], w2[c, :, cols], preferred_element_type=F32).astype(BF16).astype(F32)
        second = jnp.dot(x2[1, 0], w2[1 - c, :, cols], preferred_element_type=F32).astype(BF16).astype(F32)
        p[:, cols] = first + second
        rs[0, 0, j] = block_of(far, cols).astype(BF16)
        ring(0, 0, j).start()
        rs[1, 0, j] = block_of(far_left, cols).astype(BF16)
        ring(1, 0, j).start()

    def hop(s, carry):
        cw = lax.rem(z + half - s, chips)
        ccw = lax.rem(z + half + 1 + s, chips)
        for j in range(RCH):
            cols = pl.ds(j * width, width)
            ring(0, s - 1, j).wait_recv()
            rs[0, s, j] = (block_of(cw, cols) + rr[0, s - 1, j].astype(F32)).astype(BF16)
            ring(0, s, j).start()

            @pl.when(s < half - 1)
            def _():
                ring(1, s - 1, j).wait_recv()
                rs[1, s, j] = (block_of(ccw, cols) + rr[1, s - 1, j].astype(F32)).astype(BF16)
                ring(1, s, j).start()

        return carry

    lax.fori_loop(1, half, hop, 0)
    for j in range(RCH):
        cols = pl.ds(j * width, width)
        ring(0, half - 1, j).wait_recv()
        ring(1, half - 2, j).wait_recv()
        total = block_of(z, cols) + rr[0, half - 1, j].astype(F32) + rr[1, half - 2, j].astype(F32)
        out[:, cols] = (hidden[:, cols].astype(F32) + total).astype(BF16)

    def drain(s, carry):
        for j in range(RCH):
            ring(0, s, j).wait_send()

            @pl.when(s < half - 1)
            def _():
                ring(1, s, j).wait_send()

        return carry

    lax.fori_loop(0, half, drain, 0)


def local(
    hidden_in,
    norm_gain,
    w_query,
    w_kv,
    w_out,
    prefix_keys,
    prefix_values,
    suffix_keys,
    suffix_values,
    row_counts,
    suffix_lengths,
):
    chips = lax.axis_size("tensor_0")
    devices = 2 * chips
    my_index = lax.axis_index(TENSOR)
    own, width = hidden_in.shape
    heads = w_kv.shape[1]
    pair = w_query.shape[1]
    groups = devices // heads
    prompts = row_counts.shape[0]
    per_group = prompts // groups
    rows = suffix_lengths.shape[0]
    slab = w_kv.shape[0]
    half = chips // 2
    vmem = pl.BlockSpec(memory_space=pltpu.VMEM)
    anywhere = pl.BlockSpec(memory_space=pl.ANY)
    dma = pltpu.SemaphoreType.DMA

    slot = jnp.arange(groups * PAD, dtype=jnp.int32)
    inside = slot % PAD
    prompt = slot // PAD * per_group + inside // PCAP
    offset = inside % PCAP
    ids = jnp.arange(prompts, dtype=jnp.int32)[None, :]
    start = jnp.sum(jnp.where(ids < prompt[:, None], row_counts[None, :], 0), axis=1)
    count = jnp.sum(jnp.where(ids == prompt[:, None], row_counts[None, :], 0), axis=1)
    used = (inside < per_group * PCAP) & (offset < count)
    slot_row = jnp.where(used, start + offset, -1).astype(jnp.int32)
    mine = lax.dynamic_slice_in_dim(slot_row, my_index // heads * PAD, PAD, 0)
    hit = mine[:, None] == jnp.arange(rows, dtype=jnp.int32)[None, :]
    lens = jnp.maximum(jnp.sum(jnp.where(hit, suffix_lengths[None, :], 0), axis=1), 1).astype(jnp.int32)

    frequency = 500000.0 ** (-(2.0 * jnp.arange(HD // 2, dtype=F32)) / HD)
    angle = (PREFIX + suffix_lengths).astype(F32)[:, None] * frequency[None, :]
    cosines, sines = jnp.cos(angle), jnp.sin(angle)
    cosf = jnp.concatenate([cosines, cosines], axis=1)
    sinf = jnp.concatenate([-sines, sines], axis=1)

    q_slots, kv_slots = pl.pallas_call(
        functools.partial(project_kernel, chips),
        out_shape=(
            jax.ShapeDtypeStruct((groups, PAD, pair * HD), BF16),
            jax.ShapeDtypeStruct((PAD, 2 * HD), BF16),
        ),
        in_specs=[vmem, vmem, anywhere, anywhere, vmem, vmem, vmem],
        out_specs=(vmem, vmem),
        scratch_shapes=[
            pltpu.VMEM((devices, own, width), BF16),
            pltpu.VMEM((width, pair * HD), BF16),
            pltpu.VMEM((2 * slab, heads * 2 * HD), BF16),
            pltpu.VMEM((2, half, own, heads * 2 * HD), KVT),
            pltpu.VMEM((2, half, own, heads * 2 * HD), KVT),
            pltpu.VMEM((groups, PAD, pair * HD), BF16),
            pltpu.VMEM((heads, own, 2 * HD), BF16),
            pltpu.VMEM((devices, own, 2 * HD), BF16),
            dma, dma, dma, dma,
            dma((2, half, XCH)), dma((2, half, XCH)),
            dma((2, half + 1)), dma((2, half + 1)),
            dma((2, half)), dma((2, half)),
            dma((groups,)), dma((groups,)), dma,
            dma((devices,)), dma((devices,)), dma,
        ],
        compiler_params=pltpu.CompilerParams(collective_id=0, has_side_effects=True),
    )(
        hidden_in,
        norm_gain.reshape(1, width),
        w_query.reshape(width, pair * HD),
        w_kv.reshape(slab, heads * 2 * HD),
        cosf,
        sinf,
        slot_row.reshape(groups * PAD, 1),
    )

    keys, size = prefix_keys.shape[2], suffix_keys.shape[2]
    per = groups * pair
    attended = pl.pallas_call(
        attend_kernel,
        grid_spec=pltpu.PrefetchScalarGridSpec(
            num_scalar_prefetch=1,
            grid=(per_group,),
            in_specs=[
                pl.BlockSpec((groups, PAD, pair * HD), lambda i, s: (0, 0, 0)),
                pl.BlockSpec((PAD, 2 * HD), lambda i, s: (0, 0)),
                pl.BlockSpec((1, keys, HD), lambda i, s: (i, 0, 0)),
                pl.BlockSpec((1, keys, HD), lambda i, s: (i, 0, 0)),
                pl.BlockSpec((PCAP, size, HD), lambda i, s: (i, 0, 0)),
                pl.BlockSpec((PCAP, size, HD), lambda i, s: (i, 0, 0)),
            ],
            out_specs=pl.BlockSpec((groups, PAD, pair * HD), lambda i, s: (0, 0, 0)),
            scratch_shapes=[
                pltpu.VMEM((PAD * per, HD), F32),
                pltpu.VMEM((PAD * per, HD), F32),
                pltpu.VMEM((PAD * per, HD), F32),
                pltpu.VMEM((PCAP * per, size), F32),
                pltpu.VMEM((PCAP * per, HD), F32),
                pltpu.VMEM((PAD * per, HD), F32),
            ],
        ),
        out_shape=jax.ShapeDtypeStruct((groups, PAD, pair * HD), BF16),
        compiler_params=pltpu.CompilerParams(dimension_semantics=("arbitrary",)),
    )(lens, q_slots, kv_slots, prefix_keys[0], prefix_values[0], suffix_keys[0], suffix_values[0])

    return pl.pallas_call(
        functools.partial(output_kernel, chips),
        out_shape=jax.ShapeDtypeStruct((own, width), BF16),
        in_specs=[vmem, vmem, anywhere, vmem],
        out_specs=vmem,
        scratch_shapes=[
            pltpu.VMEM((groups, PAD, pair * HD), BF16),
            pltpu.VMEM((2, pair * HD, width), BF16),
            pltpu.VMEM((2, 2, rows // 2, pair * HD), BF16),
            pltpu.VMEM((rows // 2, width), F32),
            pltpu.VMEM((2, half, RCH, own, width // RCH), BF16),
            pltpu.VMEM((2, half, RCH, own, width // RCH), BF16),
            dma, dma, dma,
            dma((groups,)), dma((groups,)), dma,
            dma, dma,
            dma((2, half, RCH)), dma((2, half, RCH)),
        ],
        compiler_params=pltpu.CompilerParams(collective_id=1, has_side_effects=True),
    )(hidden_in, attended, w_out.reshape(pair * HD, width), slot_row.reshape(1, groups * PAD))


def solution(mesh):
    cores = 2
    split = Mesh(
        mesh.devices.reshape(mesh.shape["groups"], mesh.shape["tensor"] // cores, cores),
        ("groups", "tensor_0", "tensor_1"),
    )
    return jax.shard_map(
        local,
        mesh=split,
        in_specs=(
            P(GROUPS_TENSOR, None),
            P(),
            P(None, TENSOR, None),
            P(TENSOR, None, None, None),
            P(TENSOR, None, None),
            P(GROUPS_TENSOR, None, None, None),
            P(GROUPS_TENSOR, None, None, None),
            P(GROUPS_TENSOR, None, None, None),
            P(GROUPS_TENSOR, None, None, None),
            P("groups"),
            P("groups"),
        ),
        out_specs=P(GROUPS_TENSOR, None),
        check_vma=False,
    )
```

time: 484 us -> 163 us (0.34)
  waiting for transfers between devices: 279 us -> 0 us
  Pallas kernels: 0 us -> 146 us
  blocking collectives: 76.8 us -> 0 us
  matrix products: 50.3 us -> 0 us
  local copies, waits for them, and re-layouts: 35.8 us -> 10.6 us
  other arithmetic: 25.1 us -> 5.75 us
  between operations: 13.9 us -> 0.05 us
    all_gather x3 -> x0, waiting for transfers between devices: 179 us -> none  [the longest x1 76.1 us: local(): rows_piece = lax.all_gather(normed, TENSOR, axis=0, tiled=True)]
    pallas_call x0 -> x3, Pallas kernels: none -> 146 us  [the longest x1 72.6 us: local(): pl.pallas_call(functools.partial(project_kernel, chips), out_shape=(jax.S...]
    reduce_scatter x3 -> x0, waiting for transfers between devices: 99.4 us -> none  [sum_in_order(): blocks = lax.psum_scatter(blocks, axes[k], scatter_dimension=0, tiled=True)]
    unnamed x1 -> x0, blocking collectives: 76.8 us -> none
    dot_general x33 -> x0, matrix products: 50.3 us -> none  [the longest x6 11.3 us: attend_prompt(): jnp.einsum('rjd,rtd->rjt', query_block, tail_keys, preferred_element_type...]
    gather x6 -> x0, other arithmetic: 15.1 us -> none  [the longest x3 15.1 us: local(): row_slot = prompt_of * PCAP + (row_index - row_starts[prompt_of])]
    gather x6 -> x0, local copies, waits for them, and re-layouts: 10.5 us -> none  [the longest x1 3.61 us: local(): kv_partial[slot_flat].reshape(groups, SLOTS, KVH, 2 * HD)]
    all_gather x1 -> x0, local copies, waits for them, and re-layouts: 6.86 us -> none  [local(): complete = lax.all_gather(my_queries, TENSOR, axis=1, tiled=True)]
  transfers between devices with their start and end apart: 6 -> 0, of which waited for: 6 -> 0; matrix products, arithmetic and copies ran while one was open for 9% -> 0% of each run, Pallas kernels for 0% -> 0%
where the time goes in v1:
time: 163 us
  Pallas kernels  146 us (90%)
  local copies, waits for them, and re-layouts  10.6 us (7%)
  other arithmetic  5.75 us (4%)
    pallas_call x1, Pallas kernels, local(): pl.pallas_call(functools.partial(project_kernel, chips), out_shape=(jax.S...  72.6 us
    pallas_call x1, Pallas kernels, local(): pl.pallas_call(functools.partial(output_kernel, chips), out_shape=jax.Sha...  60.5 us
    pallas_call x1, Pallas kernels, local(): pl.pallas_call(attend_kernel, grid_spec=pltpu.PrefetchScalarGridSpec(num_...  13.3 us
    unnamed x2, local copies, waits for them, and re-layouts  6.22 us

profile of v1, /device:TPU:86, one launch (start us, length us, event | category | flops | bytes accessed | tf_op | source)
XLA Modules:
  0.0 162.7 jit_solution(12742439272853835087)
XLA Ops:
  0.0 0.7 add_convert_fusion
  0.7 0.7 select_reduce_fusion.2
  1.5 0.6 and_select_fusion.slots
  2.1 0.1 dynamic_slice.3
  2.1 0.8 select_reduce_fusion
  3.0 0.6 broadcast_maximum_fusion.lens
  3.6 1.3 reshape.172.gain
  4.9 0.1 copy.15
  5.0 0.1 copy.14
  5.2 0.9 add_select_fusion.2.slots
  6.1 0.5 fusion.9
  6.7 0.8 pad_maximum_fusion
  7.5 2.6 %reshape.174.wkv_hbm = bf16[256,2048]{1,0:T(8,128)(2,1)} reshape(bf16[256,8,2,128]{3,2,1,0:T(2,128)(2,1)} %param.14) | data formatting | bytes 2097152 | tf_op jit(solution)/shard_map/reshape | solution.py:546
  10.1 4.7 %copy.18 = bf16[1024,8,2,128]{3,1,2,0:T(8,128)(2,1)} copy(bf16[1024,8,2,128]{3,2,1,0:T(2,128)(2,1)} %bitcast.16) | data formatting | bytes 8388608
  14.8 72.6 %shard_map.109 = (bf16[4,128,256]{2,1,0:T(8,128)(2,1)}, bf16[128,256]{1,0:T(8,128)(2,1)}) custom-call(bf16[8,8192]{1,0:T(8,128)(2,1)} %hidden.3, bf16[1,8192]{1,0:T(2,128)(2,1)} %reshape.172.gain, bf16[8192,256]{1,0:T(8,128)(2,1)} %bitcast.13, bf16[256,2048]{1,0:T(8,128)(2,1)} %reshape.174.wkv_hbm, f32[256,128]{1,0:T(8,128)} %get-tuple-element.14.cosf, ...), custom_call_target="tpu_custom_call" | custom-call | tf_op jit(solution)/shard_map/pallas_call | solution.py:517
  87.4 13.3 %shard_map.110.att = bf16[4,128,256]{2,1,0:T(8,128)(2,1)} custom-call(s32[128]{0:T(128)} %broadcast_maximum_fusion.lens, bf16[4,128,256]{2,1,0:T(8,128)(2,1)} %get-tuple-element.7.q, bf16[128,256]{1,0:T(8,128)(2,1)} %get-tuple-element.8.kv, bf16[6,2048,128]{2,1,0:T(8,128)(2,1)} %bitcast.18, bf16[6,2048,128]{2,1,0:T(8,128)(2,1)} %bitcast.19, ...), custom_call_target="tpu_custom_call" | custom-call | tf_op jit(solution)/shard_map/pallas_call | solution.py:554
  100.6 60.5 %shard_map.111 = bf16[8,8192]{1,0:T(8,128)(2,1)} custom-call(bf16[8,8192]{1,0:T(8,128)(2,1)} %hidden.3, bf16[4,128,256]{2,1,0:T(8,128)(2,1)} %shard_map.110.att, bf16[256,8192]{1,0:T(8,128)(2,1)} %bitcast.17, s32[1,512]{1,0:T(1,128)} %and_select_fusion.slots), custom_call_target="tpu_custom_call" | custom-call | tf_op jit(solution)/shard_map/pallas_call | solution.py:581
  161.2 1.6 copy.20
  (3 shorter events, 0.0 us)

commit v2 on v0

v2 whole, which is shorter than its diff:
```python
import functools
import math

import jax
import jax.numpy as jnp
from jax import lax
from jax.experimental import pallas as pl
from jax.experimental.pallas import tpu as pltpu
from jax.sharding import Mesh
from jax.sharding import PartitionSpec as P

HD = 128
PREFIX = 2048
PCAP = 21
PAIR = 2
CHUNK = 48
TENSOR = ("tensor_0", "tensor_1")
GROUPS_TENSOR = ("groups", "tensor_0", "tensor_1")
MESH = pl.DeviceIdType.MESH
KVT = jnp.bfloat16
XCH = 4
RCH = 8
F32 = jnp.float32
BF16 = jnp.bfloat16
PIECE = 512


def at(z, c):
    return {"tensor_0": z, "tensor_1": c}


def remote(src, dst, send, recv, z, c):
    return pltpu.make_async_remote_copy(
        src_ref=src, dst_ref=dst, send_sem=send, recv_sem=recv, device_id=at(z, c), device_id_type=MESH
    )


def layer_kernel(
    chips, hidden, gain, wq_hbm, wkv_hbm, wo_hbm, pk_hbm, pv_hbm, sk_hbm, sv_hbm, cosf, sinf, counts, lengths, out,
    x, wq_raw, wq, wkv_raw, wkv, wide_f, kvs, kvr, qs, ql, kvh, kvl, table, starts,
    pk, pv, sk, sv, qf, kf, vf, ss, pvacc, attf, ao, a, w2, x2, p, rs, rr,
    wq_sem, wkv_sem, wkvs_sem, wkvr_sem, wo_sem, wos, wor, cache_sem,
    xs, xr, ps, pr, ks, kr, qss, qrs, qls, as_, ar, al, ass, ars, als, xss, xrs, rss, rsr,
):
    z = lax.axis_index("tensor_0")
    c = lax.axis_index("tensor_1")
    devices = 2 * chips
    half = chips // 2
    me = 2 * z + c
    right = lax.rem(z + 1, chips)
    left = lax.rem(z + chips - 1, chips)
    slab = wkv.shape[0] // 2
    features = x.shape[2]
    width = features // XCH
    rows = devices * 8
    groups, chunks = qs.shape[0], qs.shape[1]
    heads = kvh.shape[0]
    per_group = pk.shape[0]
    per = heads
    my_group = me // heads
    my_head = lax.rem(me, heads)
    scaling = 1.0 / math.sqrt(HD)
    barrier = pltpu.get_barrier_semaphore()
    for peer in ((right, c), (left, c), (z, 1 - c)):
        pl.semaphore_signal(barrier, inc=1, device_id=at(*peer), device_id_type=MESH)

    load_wkv = pltpu.make_async_copy(wkv_hbm, wkv_raw, wkv_sem)
    load_wkv.start()
    load_wq = pltpu.make_async_copy(wq_hbm, wq_raw, wq_sem)
    load_wq.start()

    wide = hidden[...].astype(F32)
    inverse = lax.rsqrt(jnp.mean(wide * wide, axis=1, keepdims=True) + 1e-05)
    for j in range(features // HD):
        cols = slice(j * HD, (j + 1) * HD)
        part = hidden[:, cols].astype(F32) * inverse * gain[j : j + 1, :].astype(F32)
        x[me, :, cols] = part.astype(BF16)
    kvs[1, 0] = jnp.zeros(kvs.shape[2:], kvs.dtype)
    own_rows = pl.ds(pl.multiple_of(c * slab, slab), slab)
    load_wkv.wait()
    columns = wkv.shape[1] // HD
    step_rows = PIECE // columns
    for n in range(slab // step_rows):
        wide_f[...] = wkv_raw[n * PIECE : (n + 1) * PIECE, :].astype(F32)
        target = pl.ds(pl.multiple_of(c * slab + n * step_rows, step_rows), step_rows)
        for i in range(columns):
            wkv[target, i * HD : (i + 1) * HD] = wide_f[pl.ds(i, step_rows, stride=columns), :].astype(BF16)

    pl.semaphore_wait(barrier, 3)

    def row_copy(way, step, j, shard):
        piece = x.at[shard, :, pl.ds(j * width, width)]
        return remote(piece, piece, xs.at[way, step, j], xr.at[way, step, j], right if way == 0 else left, c)

    def part_copy(way, step, shard):
        return remote(x.at[shard], x.at[shard], ps.at[way, step], pr.at[way, step], z, 1 - c)

    def kv_copy(way, step):
        return remote(kvs.at[way, step], kvr.at[way, step], ks.at[way, step], kr.at[way, step], right if way == 0 else left, c)

    for j in range(XCH):
        row_copy(0, 0, j, me).start()
        row_copy(1, 0, j, me).start()
    send_wkv = remote(wkv.at[own_rows, :], wkv.at[own_rows, :], wkvs_sem, wkvr_sem, z, 1 - c)
    send_wkv.start()
    part_copy(0, 0, me).start()
    kv_copy(1, 0).start()
    feats = pl.ds(pl.multiple_of(z * 2 * slab, 2 * slab), 2 * slab)

    loads = [
        pltpu.make_async_copy(pk_hbm, pk, cache_sem.at[0]),
        pltpu.make_async_copy(pv_hbm, pv, cache_sem.at[1]),
        pltpu.make_async_copy(sk_hbm, sk, cache_sem.at[2]),
        pltpu.make_async_copy(sv_hbm, sv, cache_sem.at[3]),
        pltpu.make_async_copy(wo_hbm, w2.at[c], wo_sem),
    ]

    running = jnp.int32(0)
    for n in range(groups * per_group):
        starts[n] = running
        running = running + counts[n]

    def slot_ids(g, k, shape, dim):
        index = lax.broadcasted_iota(jnp.int32, shape, dim)
        ids = jnp.full(shape, -1, jnp.int32)
        for u in range(PAIR):
            prompt = g * per_group + k * PAIR + u
            offset = index - u * PCAP
            ids = jnp.where((offset >= 0) & (offset < counts[prompt]), offset + starts[prompt], ids)
        return ids

    send_wkv.wait()
    own = jnp.dot(x[me, :, feats], wkv[...], preferred_element_type=F32)
    kvs[0, 0] = own.astype(kvs.dtype)
    kv_copy(0, 0).start()
    load_wq.wait()
    for load in loads:
        load.start()

    def relay(n):
        wide_f[...] = wq_raw[pl.ds(pl.multiple_of(n * PIECE, PIECE), PIECE), :].astype(F32)
        target = pl.ds(pl.multiple_of(n * (PIECE // 2), PIECE // 2), PIECE // 2)
        for i in range(2):
            wq[target, i * HD : (i + 1) * HD] = wide_f[pl.ds(i, PIECE // 2, stride=2), :].astype(BF16)

    pieces = 2 * features // PIECE // half
    for n in range(pieces):
        relay(n)

    def hop(s, carry):
        cw = 2 * lax.rem(z - s + chips, chips) + c
        ccw = 2 * lax.rem(z + s, chips) + c
        for j in range(XCH):
            row_copy(0, s - 1, j, cw).wait_recv()
            row_copy(0, s, j, cw).start()
            row_copy(1, s - 1, j, ccw).wait_recv()

            @pl.when(s < half - 1)
            def _():
                row_copy(1, s, j, ccw).start()

        part_copy(0, s, cw).start()
        part_copy(1, s, ccw).start()
        both = jnp.concatenate([x[cw, :, feats].astype(F32), x[ccw, :, feats].astype(F32)], axis=0).astype(BF16)
        part = jnp.dot(both, wkv[...], preferred_element_type=F32)
        kv_copy(0, s - 1).wait_recv()
        kvs[0, s] = (part[:8] + kvr[0, s - 1].astype(F32)).astype(kvs.dtype)
        kv_copy(0, s).start()
        kv_copy(1, s - 1).wait_recv()
        kvs[1, s] = (part[8:] + kvr[1, s - 1].astype(F32)).astype(kvs.dtype)
        kv_copy(1, s).start()
        for n in range(pieces):
            relay(s * pieces + n)
        return carry

    lax.fori_loop(1, half, hop, 0)
    far = 2 * lax.rem(z + half, chips) + c
    for j in range(XCH):
        row_copy(0, half - 1, j, far).wait_recv()
    part_copy(0, half, far).start()
    own = jnp.dot(x[far, :, feats], wkv[...], preferred_element_type=F32)
    kv_copy(0, half - 1).wait_recv()
    kv_copy(1, half - 1).wait_recv()
    kv_raw = (own + kvr[0, half - 1].astype(F32) + kvr[1, half - 1].astype(F32)).astype(BF16).astype(F32)
    far_rows = pl.ds(pl.multiple_of(far * 8, 8), 8)
    cos8 = cosf[far_rows, :]
    sin8 = sinf[far_rows, :]
    for h in range(heads):
        key = kv_raw[:, h * 2 * HD : h * 2 * HD + HD]
        value = kv_raw[:, h * 2 * HD + HD : (h + 1) * 2 * HD]
        kvh[h, :, :HD] = (key * cos8 + pltpu.roll(key, HD // 2, 1) * sin8).astype(BF16)
        kvh[h, :, HD:] = value.astype(BF16)

    def kv_send(n):
        return remote(kvh.at[lax.rem(n, heads)], kvl.at[far], as_.at[n], ar.at[far], n // 2, lax.rem(n, 2))

    kv_self = pltpu.make_async_copy(kvh.at[my_head], kvl.at[far], al)

    part_copy(0, 0, me).wait_recv()

    def part_wait(s, carry):
        part_copy(0, s, me).wait_recv()
        part_copy(1, s, me).wait_recv()
        return carry

    lax.fori_loop(1, half, part_wait, 0)
    part_copy(0, half, me).wait_recv()

    def kv_out_loop(n, carry):
        @pl.when(n != me)
        def _():
            kv_send(n).start()

        return carry

    lax.fori_loop(0, devices, kv_out_loop, 0)
    kv_self.start()
    depth = 1024

    def q_step(k, acc):
        piece = pl.ds(pl.multiple_of(k * depth, depth), depth)
        xk = x[:, :, piece].astype(F32).reshape(rows, depth).astype(BF16)
        return acc + jnp.dot(xk, wq[piece, :], preferred_element_type=F32)

    acc = lax.fori_loop(0, features // depth, q_step, jnp.zeros((rows, 2 * HD), F32))
    q_raw = acc.astype(BF16).astype(F32)
    roped = []
    for j in range(2):
        v = q_raw[:, j * HD : (j + 1) * HD]
        roped.append((v * cosf[...] + pltpu.roll(v, HD // 2, 1) * sinf[...]).astype(BF16))
    roped = jnp.concatenate(roped, axis=1)
    block = 2 * lax.rem(z, 2) + c

    def select(ids, dim):
        return jnp.where(lax.broadcasted_iota(jnp.int32, ids.shape, dim) == ids, 1.0, 0.0).astype(BF16)

    def q_send(g, k):
        owner = heads * g + z // 2
        return remote(qs.at[g, k], ql.at[block, k], qss.at[g, k], qrs.at[block, k], owner // 2, lax.rem(owner, 2))

    def q_local(g, k):
        return pltpu.make_async_copy(qs.at[g, k], ql.at[block, k], qls.at[k])

    for k in range(chunks):
        for g in range(groups):
            pick = select(slot_ids(g, k, (CHUNK, rows), 0), 1)
            qs[g, k] = jnp.dot(pick, roped, preferred_element_type=F32).astype(BF16)
            owner = heads * g + z // 2

            @pl.when(owner != me)
            def _():
                q_send(g, k).start()

            @pl.when(owner == me)
            def _():
                q_local(g, k).start()

    send_w = remote(wo_hbm, w2.at[c], wos, wor, z, 1 - c)
    send_w.start()
    attf[...] = jnp.zeros_like(attf)

    def kv_in_loop(n, carry):
        @pl.when(n != far)
        def _():
            remote(kvh.at[0], kvl.at[n], as_.at[0], ar.at[n], z, 1 - c).wait_recv()

        return carry

    lax.fori_loop(0, devices, kv_in_loop, 0)
    kv_self.wait()
    table[...] = kvl[...].astype(F32).reshape(rows, 2 * HD).astype(BF16)
    for load in loads:
        load.wait()

    def a_send(b, k):
        dest = groups * my_head + b
        return remote(ao.at[b, k], a.at[my_group, k], ass.at[b, k], ars.at[my_group, k], dest // 2, lax.rem(dest, 2))

    def a_local(b, k):
        return pltpu.make_async_copy(ao.at[b, k], a.at[my_group, k], als.at[k])

    span = PCAP * per
    contract = (((1,), (1,)), ((), ()))

    def attend(i, carry):
        k, u = i // PAIR, lax.rem(i, PAIR)

        @pl.when(u == 0)
        def _():
            pick = select(slot_ids(my_group, k, (CHUNK, rows), 0), 1)
            kv = jnp.dot(pick, table[...], preferred_element_type=F32)
            for j in range(per):
                kf[pl.ds(j, CHUNK, stride=per), :] = kv[:, :HD]
                vf[pl.ds(j, CHUNK, stride=per), :] = kv[:, HD:]
            for b in range(groups):
                source = groups * my_head + b

                @pl.when(source != me)
                def _():
                    remote(qs.at[0, 0], ql.at[b, k], qss.at[0, 0], qrs.at[b, k], z, 1 - c).wait_recv()

                @pl.when(source == me)
                def _():
                    q_local(0, k).wait()

            for j in range(per):
                qf[pl.ds(j, CHUNK, stride=per), :] = ql[j // 2, k, :, (j % 2) * HD : (j % 2 + 1) * HD].astype(F32)

        mine = pl.ds(pl.multiple_of(u * span, 8), span)
        qi = qf[mine, :]
        prompt = my_group * per_group + i
        first_row = starts[prompt]
        pscore = lax.dot_general(qi.astype(BF16), pk[i], contract, preferred_element_type=F32) * scaling
        for r in range(PCAP):
            q8 = qf[pl.ds(pl.multiple_of(u * span + r * per, 8), per), :].astype(BF16)
            s8 = lax.dot_general(q8, sk[i * PCAP + r], contract, preferred_element_type=F32) * scaling
            length = lengths[jnp.minimum(first_row + r, rows - 1)]
            seen = lax.broadcasted_iota(jnp.int32, s8.shape, 1) < length
            ss[r * per : (r + 1) * per, :] = jnp.where(seen, s8, -jnp.inf)
        self_score = jnp.sum(qi * kf[mine, :], axis=1, keepdims=True) * scaling
        sfx = ss[...]
        top = jnp.maximum(
            jnp.max(pscore, axis=1, keepdims=True), jnp.maximum(jnp.max(sfx, axis=1, keepdims=True), self_score)
        )
        pe = jnp.exp(pscore - top)
        se = jnp.exp(sfx - top)
        own = jnp.exp(self_score - top)
        total = jnp.sum(pe, axis=1, keepdims=True) + jnp.sum(se, axis=1, keepdims=True) + own
        acc = jnp.dot(pe.astype(BF16), pv[i], preferred_element_type=F32)
        ss[...] = se
        for r in range(PCAP):
            w8 = ss[r * per : (r + 1) * per, :].astype(BF16)
            pvacc[r * per : (r + 1) * per, :] = jnp.dot(w8, sv[i * PCAP + r], preferred_element_type=F32)
        attf[mine, :] = (acc + pvacc[...] + own * vf[mine, :]) / total

        @pl.when(u == PAIR - 1)
        def _():
            for j in range(per):
                ao[j // 2, k, :, (j % 2) * HD : (j % 2 + 1) * HD] = attf[pl.ds(j, CHUNK, stride=per), :].astype(BF16)
            for b in range(groups):
                dest = groups * my_head + b

                @pl.when(dest != me)
                def _():
                    a_send(b, k).start()

                @pl.when(dest == me)
                def _():
                    a_local(b, k).start()

        return carry

    lax.fori_loop(0, per_group, attend, 0)

    order = lax.broadcasted_iota(jnp.int32, (rows, CHUNK), 0)
    wanted = (lax.rem(order, rows // 2) // 8 * 2 + order // (rows // 2)) * 8 + lax.rem(order, 8)
    picked = jnp.zeros((rows, 2 * HD), F32)
    for k in range(chunks):
        for g in range(groups):
            source = heads * g + me // groups

            @pl.when(source != me)
            def _():
                remote(ao.at[0, 0], a.at[g, k], ass.at[0, 0], ars.at[g, k], z, 1 - c).wait_recv()

            @pl.when(source == me)
            def _():
                a_local(0, k).wait()

            pick = jnp.where(wanted == slot_ids(g, k, (rows, CHUNK), 1), 1.0, 0.0).astype(BF16)
            picked = picked + jnp.dot(pick, a[g, k], preferred_element_type=F32)
    x2[0, 0] = picked[: rows // 2].astype(BF16)
    x2[0, 1] = picked[rows // 2 :].astype(BF16)
    swap = remote(x2.at[0, 1 - c], x2.at[1, 0], xss, xrs, z, 1 - c)
    swap.start()
    send_w.wait()
    rwidth = features // RCH
    ready = 3

    def own_part(j):
        cols = pl.ds(j * rwidth, rwidth)
        p[:, cols] = jnp.dot(x2[0, c], w2[c, :, cols], preferred_element_type=F32).astype(BF16).astype(F32)

    for j in range(ready):
        own_part(j)
    swap.wait()

    def ring(way, step, j):
        return remote(
            rs.at[way, step, j], rr.at[way, step, j], rss.at[way, step, j], rsr.at[way, step, j],
            right if way == 0 else left, c,
        )

    def block_of(chip, cols):
        return p[pl.ds(pl.multiple_of(chip * 8, 8), 8), cols]

    far_chip = lax.rem(z + half, chips)
    far_left = lax.rem(z + half + 1, chips)
    for j in range(RCH):
        if j >= ready:
            own_part(j)
        cols = pl.ds(j * rwidth, rwidth)
        second = jnp.dot(x2[1, 0], w2[1 - c, :, cols], preferred_element_type=F32).astype(BF16).astype(F32)
        p[:, cols] = p[:, cols] + second
        rs[0, 0, j] = block_of(far_chip, cols).astype(BF16)
        ring(0, 0, j).start()
        rs[1, 0, j] = block_of(far_left, cols).astype(BF16)
        ring(1, 0, j).start()

    def fold(s, carry):
        cw = lax.rem(z + half - s, chips)
        ccw = lax.rem(z + half + 1 + s, chips)
        for j in range(RCH):
            cols = pl.ds(j * rwidth, rwidth)
            ring(0, s - 1, j).wait_recv()
            rs[0, s, j] = (block_of(cw, cols) + rr[0, s - 1, j].astype(F32)).astype(BF16)
            ring(0, s, j).start()

            @pl.when(s < half - 1)
            def _():
                ring(1, s - 1, j).wait_recv()
                rs[1, s, j] = (block_of(ccw, cols) + rr[1, s - 1, j].astype(F32)).astype(BF16)
                ring(1, s, j).start()

        return carry

    lax.fori_loop(1, half, fold, 0)
    for j in range(RCH):
        cols = pl.ds(j * rwidth, rwidth)
        ring(0, half - 1, j).wait_recv()
        ring(1, half - 2, j).wait_recv()
        total = block_of(z, cols) + rr[0, half - 1, j].astype(F32) + rr[1, half - 2, j].astype(F32)
        out[:, cols] = (hidden[:, cols].astype(F32) + total).astype(BF16)

    for j in range(XCH):
        row_copy(0, 0, j, me).wait_send()
        row_copy(1, 0, j, me).wait_send()
    part_copy(0, 0, me).wait_send()
    part_copy(0, half, me).wait_send()
    kv_copy(0, 0).wait_send()
    kv_copy(1, 0).wait_send()
    for j in range(RCH):
        ring(0, 0, j).wait_send()
        ring(1, 0, j).wait_send()

    def drain(s, carry):
        for j in range(XCH):
            row_copy(0, s, j, me).wait_send()

            @pl.when(s < half - 1)
            def _():
                row_copy(1, s, j, me).wait_send()

        part_copy(0, s, me).wait_send()
        part_copy(1, s, me).wait_send()
        kv_copy(0, s).wait_send()
        kv_copy(1, s).wait_send()
        for j in range(RCH):
            ring(0, s, j).wait_send()

            @pl.when(s < half - 1)
            def _():
                ring(1, s, j).wait_send()

        return carry

    lax.fori_loop(1, half, drain, 0)

    def kv_drain(n, carry):
        @pl.when(n != me)
        def _():
            kv_send(n).wait_send()

        return carry

    lax.fori_loop(0, devices, kv_drain, 0)
    for k in range(chunks):
        for g in range(groups):
            owner = heads * g + z // 2
            dest = groups * my_head + g

            @pl.when(owner != me)
            def _():
                q_send(g, k).wait_send()

            @pl.when(dest != me)
            def _():
                a_send(g, k).wait_send()


def local(
    hidden_in,
    norm_gain,
    w_query,
    w_kv,
    w_out,
    prefix_keys,
    prefix_values,
    suffix_keys,
    suffix_values,
    row_counts,
    suffix_lengths,
):
    chips = lax.axis_size("tensor_0")
    devices = 2 * chips
    own, width = hidden_in.shape
    heads = w_kv.shape[1]
    pair = w_query.shape[1]
    groups = devices // heads
    per_group = row_counts.shape[0] // groups
    chunks = per_group // PAIR
    rows = suffix_lengths.shape[0]
    slab = w_kv.shape[0]
    half = chips // 2
    keys, size = prefix_keys.shape[2], suffix_keys.shape[2]
    columns = heads * 2 * HD
    vmem = pl.BlockSpec(memory_space=pltpu.VMEM)
    smem = pl.BlockSpec(memory_space=pltpu.SMEM)
    anywhere = pl.BlockSpec(memory_space=pl.ANY)
    dma = pltpu.SemaphoreType.DMA

    frequency = 500000.0 ** (-(2.0 * (jnp.arange(HD) % (HD // 2)).astype(F32)) / HD)
    angle = (PREFIX + suffix_lengths).astype(F32)[:, None] * frequency[None, :]
    cosf = jnp.cos(angle)
    sinf = jnp.where(jnp.arange(HD) < HD // 2, -1.0, 1.0)[None, :] * jnp.sin(angle)

    slots = (groups, chunks, CHUNK, pair * HD)
    return pl.pallas_call(
        functools.partial(layer_kernel, chips),
        out_shape=jax.ShapeDtypeStruct((own, width), BF16),
        in_specs=[vmem, vmem] + [anywhere] * 7 + [vmem, vmem, smem, smem],
        out_specs=vmem,
        scratch_shapes=[
            pltpu.VMEM((devices, own, width), BF16),
            pltpu.VMEM((width * pair, HD), BF16),
            pltpu.VMEM((width, pair * HD), BF16),
            pltpu.VMEM((slab * heads * 2, HD), BF16),
            pltpu.VMEM((2 * slab, columns), BF16),
            pltpu.VMEM((PIECE, HD), F32),
            pltpu.VMEM((2, half, own, columns), KVT),
            pltpu.VMEM((2, half, own, columns), KVT),
            pltpu.VMEM(slots, BF16),
            pltpu.VMEM(slots, BF16),
            pltpu.VMEM((heads, own, 2 * HD), BF16),
            pltpu.VMEM((devices, own, 2 * HD), BF16),
            pltpu.VMEM((rows, 2 * HD), BF16),
            pltpu.SMEM((groups * per_group,), jnp.int32),
            pltpu.VMEM((per_group, keys, HD), BF16),
            pltpu.VMEM((per_group, keys, HD), BF16),
            pltpu.VMEM((per_group * PCAP, size, HD), BF16),
            pltpu.VMEM((per_group * PCAP, size, HD), BF16),
            pltpu.VMEM((CHUNK * heads, HD), F32),
            pltpu.VMEM((CHUNK * heads, HD), F32),
            pltpu.VMEM((CHUNK * heads, HD), F32),
            pltpu.VMEM((PCAP * heads, size), F32),
            pltpu.VMEM((PCAP * heads, HD), F32),
            pltpu.VMEM((CHUNK * heads, HD), F32),
            pltpu.VMEM(slots, BF16),
            pltpu.VMEM(slots, BF16),
            pltpu.VMEM((2, pair * HD, width), BF16),
            pltpu.VMEM((2, 2, rows // 2, pair * HD), BF16),
            pltpu.VMEM((rows // 2, width), F32),
            pltpu.VMEM((2, half, RCH, own, width // RCH), BF16),
            pltpu.VMEM((2, half, RCH, own, width // RCH), BF16),
            dma, dma, dma, dma, dma, dma, dma, dma((4,)),
            dma((2, half, XCH)), dma((2, half, XCH)),
            dma((2, half + 1)), dma((2, half + 1)),
            dma((2, half)), dma((2, half)),
            dma((groups, chunks)), dma((groups, chunks)), dma((chunks,)),
            dma((devices,)), dma((devices,)), dma,
            dma((groups, chunks)), dma((groups, chunks)), dma((chunks,)),
            dma, dma,
            dma((2, half, RCH)), dma((2, half, RCH)),
        ],
        compiler_params=pltpu.CompilerParams(
            collective_id=0, has_side_effects=True, vmem_limit_bytes=66_000_000
        ),
    )(
        hidden_in,
        norm_gain.reshape(width // HD, HD),
        w_query.reshape(width * pair, HD),
        w_kv.reshape(slab * heads * 2, HD),
        w_out.reshape(pair * HD, width),
        prefix_keys[0],
        prefix_values[0],
        suffix_keys[0],
        suffix_values[0],
        cosf,
        sinf,
        row_counts,
        suffix_lengths,
    )


def solution(mesh):
    cores = 2
    split = Mesh(
        mesh.devices.reshape(mesh.shape["groups"], mesh.shape["tensor"] // cores, cores),
        ("groups", "tensor_0", "tensor_1"),
    )
    return jax.shard_map(
        local,
        mesh=split,
        in_specs=(
            P(GROUPS_TENSOR, None),
            P(),
            P(None, TENSOR, None),
            P(TENSOR, None, None, None),
            P(TENSOR, None, None),
            P(GROUPS_TENSOR, None, None, None),
            P(GROUPS_TENSOR, None, None, None),
            P(GROUPS_TENSOR, None, None, None),
            P(GROUPS_TENSOR, None, None, None),
            P("groups"),
            P("groups"),
        ),
        out_specs=P(GROUPS_TENSOR, None),
        check_vma=False,
    )
```

time: 484 us -> 127 us (0.26)
  waiting for transfers between devices: 279 us -> 0 us
  Pallas kernels: 0 us -> 123 us
  blocking collectives: 76.8 us -> 0 us
  matrix products: 50.3 us -> 0 us
  local copies, waits for them, and re-layouts: 35.8 us -> 1.57 us
  other arithmetic: 25.1 us -> 1.94 us
  between operations: 13.9 us -> 0.01 us
    all_gather x3 -> x0, waiting for transfers between devices: 179 us -> none  [the longest x1 76.1 us: local(): rows_piece = lax.all_gather(normed, TENSOR, axis=0, tiled=True)]
    pallas_call x0 -> x1, Pallas kernels: none -> 123 us  [local(): pl.pallas_call(functools.partial(layer_kernel, chips), out_shape=jax.Shap...]
    reduce_scatter x3 -> x0, waiting for transfers between devices: 99.4 us -> none  [sum_in_order(): blocks = lax.psum_scatter(blocks, axes[k], scatter_dimension=0, tiled=True)]
    unnamed x1 -> x0, blocking collectives: 76.8 us -> none
    dot_general x33 -> x0, matrix products: 50.3 us -> none  [the longest x6 11.3 us: attend_prompt(): jnp.einsum('rjd,rtd->rjt', query_block, tail_keys, preferred_element_type...]
    gather x6 -> x0, other arithmetic: 15.1 us -> none  [the longest x3 15.1 us: local(): row_slot = prompt_of * PCAP + (row_index - row_starts[prompt_of])]
    gather x6 -> x0, local copies, waits for them, and re-layouts: 10.5 us -> none  [the longest x1 3.61 us: local(): kv_partial[slot_flat].reshape(groups, SLOTS, KVH, 2 * HD)]
    all_gather x1 -> x0, local copies, waits for them, and re-layouts: 6.86 us -> none  [local(): complete = lax.all_gather(my_queries, TENSOR, axis=1, tiled=True)]
  transfers between devices with their start and end apart: 6 -> 0, of which waited for: 6 -> 0; matrix products, arithmetic and copies ran while one was open for 9% -> 0% of each run, Pallas kernels for 0% -> 0%
where the time goes in v2:
time: 127 us
  Pallas kernels  123 us (97%)
  other arithmetic  1.94 us (2%)
  local copies, waits for them, and re-layouts  1.57 us (1%)
    pallas_call x1, Pallas kernels, local(): pl.pallas_call(functools.partial(layer_kernel, chips), out_shape=jax.Shap...  123 us

profile of v2, /device:TPU:86, one launch (start us, length us, event | category | flops | bytes accessed | tf_op | source)
XLA Modules:
  0.0 126.7 jit_solution(17907769743543290998)
XLA Ops:
  0.0 0.7 add_convert_fusion
  0.7 1.2 fusion
  1.9 123.2 %shard_map.109 = bf16[8,8192]{1,0:T(8,128)(2,1)} custom-call(bf16[8,8192]{1,0:T(8,128)(2,1)} %hidden.1, bf16[64,128]{1,0:T(8,128)(2,1)} %bitcast.15, bf16[16384,128]{1,0:T(8,128)(2,1)} %bitcast.10, bf16[4096,128]{1,0:T(8,128)(2,1)} %bitcast.14, bf16[256,8192]{1,0:T(8,128)(2,1)} %bitcast.11, bf16[6,2048,128]{2,1,0:T(8,128)(2,1)} %bitcast.12, ...), custom_call_target="tpu_custom_call" | custom-call | tf_op jit(solution)/shard_map/pallas_call | solution.py:528
  125.1 1.6 %copy.13 = bf16[8,8192]{1,0:T(8,128)(2,1)} copy(bf16[8,8192]{1,0:T(8,128)(2,1)} %shard_map.109) | data formatting | bytes 262144
  (1 shorter events, 0.0 us)

commit v3 on v2

--- a/solution.py
+++ b/solution.py
@@ -12,8 +12,8 @@
 HD = 128
 PREFIX = 2048
 PCAP = 21
-PAIR = 2
-CHUNK = 48
+PAIR = 3
+CHUNK = 64
 TENSOR = ("tensor_0", "tensor_1")
 GROUPS_TENSOR = ("groups", "tensor_0", "tensor_1")
 MESH = pl.DeviceIdType.MESH
@@ -38,7 +38,7 @@
 def layer_kernel(
     chips, hidden, gain, wq_hbm, wkv_hbm, wo_hbm, pk_hbm, pv_hbm, sk_hbm, sv_hbm, cosf, sinf, counts, lengths, out,
     x, wq_raw, wq, wkv_raw, wkv, wide_f, kvs, kvr, qs, ql, kvh, kvl, table, starts,
-    pk, pv, sk, sv, qf, kf, vf, ss, pvacc, attf, ao, a, w2, x2, p, rs, rr,
+    pk, pv, sk, sv, qf, kf, vf, mf, lf, qt, qacc, ss, pvacc, attf, ao, a, w2, x2, p, rs, rr,
     wq_sem, wkv_sem, wkvs_sem, wkvr_sem, wo_sem, wos, wor, cache_sem,
     xs, xr, ps, pr, ks, kr, qss, qrs, qls, as_, ar, al, ass, ars, als, xss, xrs, rss, rsr,
 ):
@@ -75,6 +75,22 @@
         cols = slice(j * HD, (j + 1) * HD)
         part = hidden[:, cols].astype(F32) * inverse * gain[j : j + 1, :].astype(F32)
         x[me, :, cols] = part.astype(BF16)
+    pl.semaphore_wait(barrier, 3)
+
+    def row_copy(way, step, j, shard):
+        piece = x.at[shard, :, pl.ds(j * width, width)]
+        return remote(piece, piece, xs.at[way, step, j], xr.at[way, step, j], right if way == 0 else left, c)
+
+    def part_copy(way, step, shard):
+        return remote(x.at[shard], x.at[shard], ps.at[way, step], pr.at[way, step], z, 1 - c)
+
+    def kv_copy(way, step):
+        return remote(kvs.at[way, step], kvr.at[way, step], ks.at[way, step], kr.at[way, step], right if way == 0 else left, c)
+
+    for j in range(XCH):
+        row_copy(0, 0, j, me).start()
+        row_copy(1, 0, j, me).start()
+    part_copy(0, 0, me).start()
     kvs[1, 0] = jnp.zeros(kvs.shape[2:], kvs.dtype)
     own_rows = pl.ds(pl.multiple_of(c * slab, slab), slab)
     load_wkv.wait()
@@ -86,24 +102,8 @@
         for i in range(columns):
             wkv[target, i * HD : (i + 1) * HD] = wide_f[pl.ds(i, step_rows, stride=columns), :].astype(BF16)
 
-    pl.semaphore_wait(barrier, 3)
-
-    def row_copy(way, step, j, shard):
-        piece = x.at[shard, :, pl.ds(j * width, width)]
-        return remote(piece, piece, xs.at[way, step, j], xr.at[way, step, j], right if way == 0 else left, c)
-
-    def part_copy(way, step, shard):
-        return remote(x.at[shard], x.at[shard], ps.at[way, step], pr.at[way, step], z, 1 - c)
-
-    def kv_copy(way, step):
-        return remote(kvs.at[way, step], kvr.at[way, step], ks.at[way, step], kr.at[way, step], right if way == 0 else left, c)
-
-    for j in range(XCH):
-        row_copy(0, 0, j, me).start()
-        row_copy(1, 0, j, me).start()
     send_wkv = remote(wkv.at[own_rows, :], wkv.at[own_rows, :], wkvs_sem, wkvr_sem, z, 1 - c)
     send_wkv.start()
-    part_copy(0, 0, me).start()
     kv_copy(1, 0).start()
     feats = pl.ds(pl.multiple_of(z * 2 * slab, 2 * slab), 2 * slab)
 
@@ -143,41 +143,143 @@
         for i in range(2):
             wq[target, i * HD : (i + 1) * HD] = wide_f[pl.ds(i, PIECE // 2, stride=2), :].astype(BF16)
 
-    pieces = 2 * features // PIECE // half
+    early = half // 2
+    pieces = 2 * features // PIECE // early
+    each = pieces // XCH
     for n in range(pieces):
         relay(n)
+
+    def part_wait(s):
+        part_copy(0, s, me).wait_recv()
+        part_copy(1, s, me).wait_recv()
+
+    def kv_step(s):
+        cw = 2 * lax.rem(z - s + chips, chips) + c
+        ccw = 2 * lax.rem(z + s, chips) + c
+        both = jnp.concatenate([x[cw, :, feats].astype(F32), x[ccw, :, feats].astype(F32)], axis=0).astype(BF16)
+        part = jnp.dot(both, wkv[...], preferred_element_type=F32)
+        for way in range(2):
+            kv_copy(way, s - 1).wait_recv()
+            kvs[way, s] = (part[8 * way : 8 * way + 8] + kvr[way, s - 1].astype(F32)).astype(kvs.dtype)
+            kv_copy(way, s).start()
+
+    def shard_of(index, core):
+        return 2 * lax.rem(index + 2 * chips, chips) + core
+
+    def project(shards, j):
+        cols = pl.ds(j * width, width)
+        stacked = jnp.concatenate([x[n, :, cols].astype(F32) for n in shards], axis=0).astype(BF16)
+        part = jnp.dot(stacked, wq[j * width : (j + 1) * width, :], preferred_element_type=F32)
+        size = len(shards) * 8
+        if j == 0:
+            qacc[:size] = part
+        else:
+            qacc[:size] = qacc[:size] + part
+        if j == XCH - 1:
+            for n, shard in enumerate(shards):
+                qt[pl.ds(pl.multiple_of(shard * 8, 8), 8), :] = qacc[n * 8 : n * 8 + 8]
 
     def hop(s, carry):
         cw = 2 * lax.rem(z - s + chips, chips) + c
         ccw = 2 * lax.rem(z + s, chips) + c
+
+        @pl.when(s == early)
+        def _():
+            part_copy(0, 0, me).wait_recv()
+            part_wait(1)
+
+        @pl.when(s == early + 1)
+        def _():
+            part_wait(2)
+            part_wait(3)
+
+        @pl.when(s == early + 2)
+        def _():
+            part_wait(4)
+            part_wait(5)
+
+        @pl.when(s == early + 3)
+        def _():
+            part_wait(6)
+
+        late = jnp.minimum(2 * (s - early), half - 2)
+        later = jnp.minimum(late + 1, half - 2)
         for j in range(XCH):
             row_copy(0, s - 1, j, cw).wait_recv()
-            row_copy(0, s, j, cw).start()
+
+            @pl.when((s < half - 1) | (j < XCH // 2))
+            def _():
+                row_copy(0, s, j, cw).start()
+
             row_copy(1, s - 1, j, ccw).wait_recv()
 
-            @pl.when(s < half - 1)
+            @pl.when((s < half - 1) | (j >= XCH // 2))
             def _():
                 row_copy(1, s, j, ccw).start()
 
-        part_copy(0, s, cw).start()
-        part_copy(1, s, ccw).start()
-        both = jnp.concatenate([x[cw, :, feats].astype(F32), x[ccw, :, feats].astype(F32)], axis=0).astype(BF16)
-        part = jnp.dot(both, wkv[...], preferred_element_type=F32)
-        kv_copy(0, s - 1).wait_recv()
-        kvs[0, s] = (part[:8] + kvr[0, s - 1].astype(F32)).astype(kvs.dtype)
-        kv_copy(0, s).start()
-        kv_copy(1, s - 1).wait_recv()
-        kvs[1, s] = (part[8:] + kvr[1, s - 1].astype(F32)).astype(kvs.dtype)
-        kv_copy(1, s).start()
-        for n in range(pieces):
-            relay(s * pieces + n)
+            if j == XCH - 1:
+                part_copy(0, s, cw).start()
+                part_copy(1, s, ccw).start()
+
+            @pl.when(s < early)
+            def _():
+                for n in range(each):
+                    relay(s * pieces + j * each + n)
+
+            @pl.when(s >= early)
+            def _():
+                project([shard_of(z + way * n, core) for n in (late, later) for way in (-1, 1) for core in (0, 1)], j)
+
+            if j == XCH - 1:
+                kv_step(s)
+
         return carry
 
     lax.fori_loop(1, half, hop, 0)
     far = 2 * lax.rem(z + half, chips) + c
     for j in range(XCH):
-        row_copy(0, half - 1, j, far).wait_recv()
+        row_copy(0 if j < XCH // 2 else 1, half - 1, j, far).wait_recv()
     part_copy(0, half, far).start()
+    block = 2 * lax.rem(z, 2) + c
+    part_wait(half - 1)
+    last = [shard_of(z + way * (half - 1), core) for way in (-1, 1) for core in (0, 1)] + [far]
+    part_copy(0, half, me).wait_recv()
+    last.append(2 * lax.rem(z + half, chips) + 1 - c)
+    for j in range(XCH):
+        project(last, j)
+    q_raw = qt[...].astype(BF16).astype(F32)
+    roped = []
+    for j in range(2):
+        v = q_raw[:, j * HD : (j + 1) * HD]
+        roped.append((v * cosf[...] + pltpu.roll(v, HD // 2, 1) * sinf[...]).astype(BF16))
+    roped = jnp.concatenate(roped, axis=1)
+
+    def select(ids, dim):
+        return jnp.where(lax.broadcasted_iota(jnp.int32, ids.shape, dim) == ids, 1.0, 0.0).astype(BF16)
+
+    def q_send(g, k):
+        owner = heads * g + z // 2
+        return remote(qs.at[g, k], ql.at[block, k], qss.at[g, k], qrs.at[block, k], owner // 2, lax.rem(owner, 2))
+
+    def q_local(g, k):
+        return pltpu.make_async_copy(qs.at[g, k], ql.at[block, k], qls.at[k])
+
+    def q_out(k):
+        for turn in (2, 1, 3, 0):
+            g = lax.rem(z // (chips // groups) + turn, groups)
+            pick = select(slot_ids(g, k, (CHUNK, rows), 0), 1)
+            qs[g, k] = jnp.dot(pick, roped, preferred_element_type=F32).astype(BF16)
+            owner = heads * g + z // 2
+
+            @pl.when(owner != me)
+            def _():
+                q_send(g, k).start()
+
+            @pl.when(owner == me)
+            def _():
+                q_local(g, k).start()
+
+    q_out(0)
     own = jnp.dot(x[far, :, feats], wkv[...], preferred_element_type=F32)
     kv_copy(0, half - 1).wait_recv()
     kv_copy(1, half - 1).wait_recv()
@@ -196,68 +298,27 @@
 
     kv_self = pltpu.make_async_copy(kvh.at[my_head], kvl.at[far], al)
 
-    part_copy(0, 0, me).wait_recv()
-
-    def part_wait(s, carry):
-        part_copy(0, s, me).wait_recv()
-        part_copy(1, s, me).wait_recv()
+    def kv_out_loop(i, carry):
+        ahead = lax.rem(me + chips + i, devices)
+        behind = lax.rem(me + chips - i + devices, devices)
+        kv_send(ahead).start()
+
+        @pl.when(i > 0)
+        def _():
+            kv_send(behind).start()
+
         return carry
 
-    lax.fori_loop(1, half, part_wait, 0)
-    part_copy(0, half, me).wait_recv()
-
-    def kv_out_loop(n, carry):
-        @pl.when(n != me)
-        def _():
-            kv_send(n).start()
-
-        return carry
-
-    lax.fori_loop(0, devices, kv_out_loop, 0)
+    lax.fori_loop(0, chips, kv_out_loop, 0)
     kv_self.start()
-    depth = 1024
-
-    def q_step(k, acc):
-        piece = pl.ds(pl.multiple_of(k * depth, depth), depth)
-        xk = x[:, :, piece].astype(F32).reshape(rows, depth).astype(BF16)
-        return acc + jnp.dot(xk, wq[piece, :], preferred_element_type=F32)
-
-    acc = lax.fori_loop(0, features // depth, q_step, jnp.zeros((rows, 2 * HD), F32))
-    q_raw = acc.astype(BF16).astype(F32)
-    roped = []
-    for j in range(2):
-        v = q_raw[:, j * HD : (j + 1) * HD]
-        roped.append((v * cosf[...] + pltpu.roll(v, HD // 2, 1) * sinf[...]).astype(BF16))
-    roped = jnp.concatenate(roped, axis=1)
-    block = 2 * lax.rem(z, 2) + c
-
-    def select(ids, dim):
-        return jnp.where(lax.broadcasted_iota(jnp.int32, ids.shape, dim) == ids, 1.0, 0.0).astype(BF16)
-
-    def q_send(g, k):
-        owner = heads * g + z // 2
-        return remote(qs.at[g, k], ql.at[block, k], qss.at[g, k], qrs.at[block, k], owner // 2, lax.rem(owner, 2))
-
-    def q_local(g, k):
-        return pltpu.make_async_copy(qs.at[g, k], ql.at[block, k], qls.at[k])
-
-    for k in range(chunks):
-        for g in range(groups):
-            pick = select(slot_ids(g, k, (CHUNK, rows), 0), 1)
-            qs[g, k] = jnp.dot(pick, roped, preferred_element_type=F32).astype(BF16)
-            owner = heads * g + z // 2
-
-            @pl.when(owner != me)
-            def _():
-                q_send(g, k).start()
-
-            @pl.when(owner == me)
-            def _():
-                q_local(g, k).start()
+    for k in range(1, chunks):
+        q_out(k)
 
     send_w = remote(wo_hbm, w2.at[c], wos, wor, z, 1 - c)
     send_w.start()
     attf[...] = jnp.zeros_like(attf)
+    mf[...] = jnp.zeros_like(mf)
+    lf[...] = jnp.zeros_like(lf)
 
     def kv_in_loop(n, carry):
         @pl.when(n != far)
@@ -266,9 +327,6 @@
 
         return carry
 
-    lax.fori_loop(0, devices, kv_in_loop, 0)
-    kv_self.wait()
-    table[...] = kvl[...].astype(F32).reshape(rows, 2 * HD).astype(BF16)
     for load in loads:
         load.wait()
 
@@ -287,11 +345,6 @@
 
         @pl.when(u == 0)
         def _():
-            pick = select(slot_ids(my_group, k, (CHUNK, rows), 0), 1)
-            kv = jnp.dot(pick, table[...], preferred_element_type=F32)
-            for j in range(per):
-                kf[pl.ds(j, CHUNK, stride=per), :] = kv[:, :HD]
-                vf[pl.ds(j, CHUNK, stride=per), :] = kv[:, HD:]
             for b in range(groups):
                 source = groups * my_head + b
 
@@ -317,24 +370,38 @@
             length = lengths[jnp.minimum(first_row + r, rows - 1)]
             seen = lax.broadcasted_iota(jnp.int32, s8.shape, 1) < length
             ss[r * per : (r + 1) * per, :] = jnp.where(seen, s8, -jnp.inf)
-        self_score = jnp.sum(qi * kf[mine, :], axis=1, keepdims=True) * scaling
         sfx = ss[...]
-        top = jnp.maximum(
-            jnp.max(pscore, axis=1, keepdims=True), jnp.maximum(jnp.max(sfx, axis=1, keepdims=True), self_score)
-        )
+        top = jnp.maximum(jnp.max(pscore, axis=1, keepdims=True), jnp.max(sfx, axis=1, keepdims=True))
         pe = jnp.exp(pscore - top)
         se = jnp.exp(sfx - top)
-        own = jnp.exp(self_score - top)
-        total = jnp.sum(pe, axis=1, keepdims=True) + jnp.sum(se, axis=1, keepdims=True) + own
+        mf[mine, :] = jnp.broadcast_to(top, (span, HD))
+        total = jnp.sum(pe, axis=1, keepdims=True) + jnp.sum(se, axis=1, keepdims=True)
+        lf[mine, :] = jnp.broadcast_to(total, (span, HD))
         acc = jnp.dot(pe.astype(BF16), pv[i], preferred_element_type=F32)
         ss[...] = se
         for r in range(PCAP):
             w8 = ss[r * per : (r + 1) * per, :].astype(BF16)
             pvacc[r * per : (r + 1) * per, :] = jnp.dot(w8, sv[i * PCAP + r], preferred_element_type=F32)
-        attf[mine, :] = (acc + pvacc[...] + own * vf[mine, :]) / total
+        attf[mine, :] = acc + pvacc[...]
+
+        @pl.when(i == PAIR - 1)
+        def _():
+            lax.fori_loop(0, devices, kv_in_loop, 0)
+            kv_self.wait()
+            table[...] = kvl[...].astype(F32).reshape(rows, 2 * HD).astype(BF16)
 
         @pl.when(u == PAIR - 1)
         def _():
+            pick = select(slot_ids(my_group, k, (CHUNK, rows), 0), 1)
+            kv = jnp.dot(pick, table[...], preferred_element_type=F32)
+            for j in range(per):
+                kf[pl.ds(j, CHUNK, stride=per), :] = kv[:, :HD]
+                vf[pl.ds(j, CHUNK, stride=per), :] = kv[:, HD:]
+            self_score = jnp.sum(qf[...] * kf[...], axis=1, keepdims=True) * scaling
+            peak = jnp.maximum(mf[...], self_score)
+            past = jnp.exp(mf[...] - peak)
+            own = jnp.exp(self_score - peak)
+            attf[...] = (attf[...] * past + own * vf[...]) / (lf[...] * past + own)
             for j in range(per):
                 ao[j // 2, k, :, (j % 2) * HD : (j % 2 + 1) * HD] = attf[pl.ds(j, CHUNK, stride=per), :].astype(BF16)
             for b in range(groups):
@@ -394,42 +461,44 @@
     def block_of(chip, cols):
         return p[pl.ds(pl.multiple_of(chip * 8, 8), 8), cols]
 
-    far_chip = lax.rem(z + half, chips)
-    far_left = lax.rem(z + half + 1, chips)
+    def dest_of(way, s):
+        return lax.rem(z + half - s, chips) if way == 0 else lax.rem(z + half + s, chips)
+
+    def starts_far(way, j):
+        return (j < RCH // 2) == (way == 0)
+
     for j in range(RCH):
         if j >= ready:
             own_part(j)
         cols = pl.ds(j * rwidth, rwidth)
         second = jnp.dot(x2[1, 0], w2[1 - c, :, cols], preferred_element_type=F32).astype(BF16).astype(F32)
         p[:, cols] = p[:, cols] + second
-        rs[0, 0, j] = block_of(far_chip, cols).astype(BF16)
-        ring(0, 0, j).start()
-        rs[1, 0, j] = block_of(far_left, cols).astype(BF16)
-        ring(1, 0, j).start()
+        for way in range(2):
+            step = 0 if starts_far(way, j) else 1
+            rs[way, step, j] = block_of(dest_of(way, step), cols).astype(BF16)
+            ring(way, step, j).start()
+
+    def fold_one(way, s, j):
+        cols = pl.ds(j * rwidth, rwidth)
+        ring(way, s - 1, j).wait_recv()
+        rs[way, s, j] = (block_of(dest_of(way, s), cols) + rr[way, s - 1, j].astype(F32)).astype(BF16)
+        ring(way, s, j).start()
+
+    for j in range(RCH):
+        fold_one(0 if starts_far(0, j) else 1, 1, j)
 
     def fold(s, carry):
-        cw = lax.rem(z + half - s, chips)
-        ccw = lax.rem(z + half + 1 + s, chips)
         for j in range(RCH):
-            cols = pl.ds(j * rwidth, rwidth)
-            ring(0, s - 1, j).wait_recv()
-            rs[0, s, j] = (block_of(cw, cols) + rr[0, s - 1, j].astype(F32)).astype(BF16)
-            ring(0, s, j).start()
-
-            @pl.when(s < half - 1)
-            def _():
-                ring(1, s - 1, j).wait_recv()
-                rs[1, s, j] = (block_of(ccw, cols) + rr[1, s - 1, j].astype(F32)).astype(BF16)
-                ring(1, s, j).start()
-
+            fold_one(0, s, j)
+            fold_one(1, s, j)
         return carry
 
-    lax.fori_loop(1, half, fold, 0)
+    lax.fori_loop(2, half, fold, 0)
     for j in range(RCH):
         cols = pl.ds(j * rwidth, rwidth)
         ring(0, half - 1, j).wait_recv()
-        ring(1, half - 2, j).wait_recv()
-        total = block_of(z, cols) + rr[0, half - 1, j].astype(F32) + rr[1, half - 2, j].astype(F32)
+        ring(1, half - 1, j).wait_recv()
+        total = block_of(z, cols) + rr[0, half - 1, j].astype(F32) + rr[1, half - 1, j].astype(F32)
         out[:, cols] = (hidden[:, cols].astype(F32) + total).astype(BF16)
 
     for j in range(XCH):
@@ -440,14 +509,16 @@
     kv_copy(0, 0).wait_send()
     kv_copy(1, 0).wait_send()
     for j in range(RCH):
-        ring(0, 0, j).wait_send()
-        ring(1, 0, j).wait_send()
+        ring(0 if starts_far(0, j) else 1, 0, j).wait_send()
 
     def drain(s, carry):
         for j in range(XCH):
-            row_copy(0, s, j, me).wait_send()
-
-            @pl.when(s < half - 1)
+
+            @pl.when((s < half - 1) | (j < XCH // 2))
+            def _():
+                row_copy(0, s, j, me).wait_send()
+
+            @pl.when((s < half - 1) | (j >= XCH // 2))
             def _():
                 row_copy(1, s, j, me).wait_send()
 
@@ -457,10 +528,7 @@
         kv_copy(1, s).wait_send()
         for j in range(RCH):
             ring(0, s, j).wait_send()
-
-            @pl.when(s < half - 1)
-            def _():
-                ring(1, s, j).wait_send()
+            ring(1, s, j).wait_send()
 
         return carry
 
@@ -552,6 +620,10 @@
             pltpu.VMEM((CHUNK * heads, HD), F32),
             pltpu.VMEM((CHUNK * heads, HD), F32),
             pltpu.VMEM((CHUNK * heads, HD), F32),
+            pltpu.VMEM((CHUNK * heads, HD), F32),
+            pltpu.VMEM((CHUNK * heads, HD), F32),
+            pltpu.VMEM((rows, pair * HD), F32),
+            pltpu.VMEM((8 * own, pair * HD), F32),
             pltpu.VMEM((PCAP * heads, size), F32),
             pltpu.VMEM((PCAP * heads, HD), F32),
             pltpu.VMEM((CHUNK * heads, HD), F32),

time: 127 us -> 125 us (0.984)
    pallas_call x1, Pallas kernels: 123 us -> 122 us  [local(): pl.pallas_call(functools.partial(layer_kernel, chips), out_shape=jax.Shap...]
where the time goes in v3:
time: 125 us
  Pallas kernels  122 us (98%)
  other arithmetic  1.94 us (2%)
  local copies, waits for them, and re-layouts  1.57 us (1%)
    pallas_call x1, Pallas kernels, local(): pl.pallas_call(functools.partial(layer_kernel, chips), out_shape=jax.Shap...  122 us

profile of v3, /device:TPU:86, one launch (start us, length us, event | category | flops | bytes accessed | tf_op | source)
XLA Modules:
  0.0 125.2 jit_solution(6408182332357929695)
XLA Ops:
  0.0 0.7 add_convert_fusion
  0.7 1.2 fusion
  1.9 121.6 %shard_map.109 = bf16[8,8192]{1,0:T(8,128)(2,1)} custom-call(bf16[8,8192]{1,0:T(8,128)(2,1)} %hidden.1, bf16[64,128]{1,0:T(8,128)(2,1)} %bitcast.15, bf16[16384,128]{1,0:T(8,128)(2,1)} %bitcast.10, bf16[4096,128]{1,0:T(8,128)(2,1)} %bitcast.14, bf16[256,8192]{1,0:T(8,128)(2,1)} %bitcast.11, bf16[6,2048,128]{2,1,0:T(8,128)(2,1)} %bitcast.12, ...), custom_call_target="tpu_custom_call" | custom-call | tf_op jit(solution)/shard_map/pallas_call | solution.py:596
  123.6 1.6 %copy.13 = bf16[8,8192]{1,0:T(8,128)(2,1)} copy(bf16[8,8192]{1,0:T(8,128)(2,1)} %shard_map.109) | data formatting | bytes 262144
  (1 shorter events, 0.0 us)
